TPU v7x, 128 devices: a whole 4x4x4 slice. The times are simulated.
128 devices in a mesh: ga: 16 (over x, z_hi, core), ba: 8 (over y, z_lo).
Axes of the slice: x: 4, y: 4, z: 4 (z_hi: 2, z_lo: 2; z = z_hi * 2 + z_lo), core: 2. Of those that a mesh axis runs over, the one named last changes fastest.
Arguments:
- psi: float32 [2, 32768, 2048], P(None, 'ga', 'ba'), may hold values from -0.15625 to 0.15625
- dpsi: float32 [2, 32768, 512], P(None, 'ga', 'ba'), may hold values from -6 to 6
- band_weight: float32 [2048], replicated, may hold values from 0.25 to 1
- panel_band: int32 [16], P('ba'), may hold values from 0 to 15, each once
- slab_offset: int32 [16], replicated, may hold values from 0 to 2047
Outputs:
- projected: float32 [2, 32768, 512], P(None, 'ga', 'ba')
Inputs may be any that keep to these rules, and one draw needn't show every extreme that they name: panel_band is a permutation of the panel numbers.
All inputs are finite; a program needn't handle non-finite values.
Results may differ from a plain program's by a relative error of at most 0.00012.
Values sent between devices are 32-bit elements; how exact they have to be, the bound alone decides.
A program may use at most 128 MiB of HBM per device.

v0:
```python
import jax
import jax.numpy as jnp
from jax import lax
from jax.experimental import pallas as pl
from jax.experimental.pallas import tpu as pltpu
from jax.sharding import PartitionSpec as P

F32, BF16 = jnp.float32, jnp.bfloat16
PANEL = 128
SLAB = 2048
HALF = SLAB // 2
BANDS = 256
COLS = 128
CHUNK = 256
NC = HALF // CHUNK
NT = (((1,), (1,)), ((), ()))


def split(value):
    high = value.astype(BF16)
    return high, (value - high.astype(F32)).astype(BF16)


def three(dot, left, right):
    return dot(left[0], right[0]) + (dot(left[0], right[1]) + dot(left[1], right[0]))


def nn(left, right):
    return jnp.dot(left, right, preferred_element_type=F32)


def nt(left, right):
    return lax.dot_general(left, right, NT, preferred_element_type=F32)


def kernel(
    at, psi, wt, out,
    psi_o, psi_p, a_v, a_hi, a_lo, p_hi, p_lo, wv, m, w, c,
    r0, r1, r2, s, rl, fin, zin,
    local_sem, a_s, a_r, p_s, p_r, g_s, g_r, c_s, c_r,
):
    ga, ba = lax.axis_index("ga"), lax.axis_index("ba")
    x, zhi, core = ga // 4, (ga // 2) % 2, ga % 2
    y, o = ba // 2, ba % 2
    p = 1 - o
    z = zhi * 2 + o
    oc = 1 - core

    def device(x=x, z=z, y=y, core=core):
        return (x * 4 + (z // 2) * 2 + core, y * 2 + z % 2)

    pair = device(z=zhi * 2 + p)
    up, down = device(y=(y + 1) % 4), device(y=(y + 3) % 4)
    other = device(core=oc)
    along_x = [device(x=(x + k) % 4) for k in (1, 2, 3)]
    along_z = [device(z=(z + k) % 4) for k in (1, 2, 3)]

    sent = []

    def send(src, dst, sems, index, to):
        copy = pltpu.make_async_remote_copy(
            src_ref=src, dst_ref=dst, send_sem=sems[0].at[index], recv_sem=sems[1].at[index],
            device_id=to, device_id_type=pl.DeviceIdType.MESH,
        )
        copy.start()
        sent.append(copy)
        return copy

    local = pltpu.make_async_copy(
        psi.at[:, pl.ds(pl.multiple_of(o * HALF, HALF), HALF), :], psi_o, local_sem
    )
    local.start()

    barrier = pltpu.get_barrier_semaphore()
    peers = [up, down, other, *along_x, *along_z]
    for peer in peers:
        pl.semaphore_signal(barrier, inc=1, device_id=peer, device_id_type=pl.DeviceIdType.MESH)
    pl.semaphore_wait(barrier, len(peers))

    A = (a_s, a_r)
    mine = at.at[:, pl.ds(pl.multiple_of(o * HALF, HALF), HALF)]
    theirs = at.at[:, pl.ds(pl.multiple_of(p * HALF, HALF), HALF)]
    a_pair = send(theirs, a_v.at[3, o], A, 0, pair)
    w_pair = send(wt, wv.at[o], A, 7, pair)
    a_up_o = send(mine, a_v.at[2, o], A, 1, up)
    a_down_o = send(mine, a_v.at[1, o], A, 2, down)
    waves = [
        send(
            psi.at[:, pl.ds(pl.multiple_of(p * HALF + k * CHUNK, CHUNK), CHUNK), :],
            psi_p.at[:, pl.ds(k * CHUNK, CHUNK), :], (p_s, p_r), k, pair,
        )
        for k in range(NC)
    ]

    def keep_columns(value, rel, half):
        rows = rel * 256 + half * COLS
        top = pl.ds(pl.multiple_of(rows, 64), 64)
        bottom = pl.ds(pl.multiple_of(rows + 64, 64), 64)
        for ref, part in zip((a_hi, a_lo), split(value)):
            ref[top, :HALF] = part[:64]
            ref[bottom, :HALF] = part[64:]
            ref[top, HALF:] = part[64:]
            ref[bottom, HALF:] = -part[:64]

    def keep_waves(ref, half, first, count):
        def body(k, _):
            rows = pl.ds(pl.multiple_of(first + k * CHUNK, CHUNK), CHUNK)
            for part in (0, 1):
                high, low = split(ref[part, rows, :])
                at_rows = pl.ds(pl.multiple_of(part * HALF + first + k * CHUNK, CHUNK), CHUNK)
                p_hi[half, at_rows, :] = high
                p_lo[half, at_rows, :] = low
            return 0

        lax.fori_loop(0, count, body, 0)

    wv[o] = wt[...]
    keep_columns(at[:, pl.ds(pl.multiple_of(o * HALF, HALF), HALF)], 3, o)
    local.wait()
    keep_waves(psi_o, o, 0, NC)

    a_pair.wait_recv()
    a_up_p = send(a_v.at[3, p], a_v.at[2, p], A, 3, up)
    a_down_p = send(a_v.at[3, p], a_v.at[1, p], A, 4, down)
    a_up_o.wait_recv()
    far_o = send(a_v.at[2, o], a_v.at[0, o], A, 5, up)
    keep_columns(a_v[3, p], 3, p)
    keep_columns(a_v[2, o], 2, o)
    a_down_o.wait_recv()
    keep_columns(a_v[1, o], 1, o)
    a_down_p.wait_recv()
    far_p = send(a_v.at[1, p], a_v.at[0, p], A, 6, down)
    keep_columns(a_v[1, p], 1, p)
    a_up_p.wait_recv()
    keep_columns(a_v[2, p], 2, p)
    waves[0].wait_recv()
    keep_waves(psi_p, p, 0, 1)
    far_o.wait_recv()
    keep_columns(a_v[0, o], 0, o)
    far_p.wait_recv()
    keep_columns(a_v[0, p], 0, p)
    w_pair.wait_recv()

    def own_bands(rel, _):
        rows = pl.ds(pl.multiple_of(rel * 256, 256), 256)
        left = (a_hi[rows, :], a_lo[rows, :])
        m[o, rows, :] = three(nn, left, (p_hi[o], p_lo[o]))
        return 0

    lax.fori_loop(0, 4, own_bands, 0)

    def pair_bands(rel, k):
        rows = pl.ds(rel * 256, 256) if isinstance(rel, int) else pl.ds(pl.multiple_of(rel * 256, 256), 256)
        total = None if k == 0 else m[p, rows, :]
        for first in (k * CHUNK, HALF + k * CHUNK):
            ks = pl.ds(first, CHUNK)
            term = three(
                nn, (a_hi[rows, ks], a_lo[rows, ks]), (p_hi[p, ks, :], p_lo[p, ks, :])
            )
            total = term if total is None else total + term
        m[p, rows, :] = total

    def pair_bands_all(k):
        def body(rel, _):
            pair_bands(rel, k)
            return 0

        lax.fori_loop(0, 4, body, 0)

    pair_bands_all(0)
    for k in range(1, NC):
        waves[k].wait_recv()
        keep_waves(psi_p, p, k * CHUNK, 1)
        if k < NC - 1:
            pair_bands_all(k)

    G = (g_s, g_r)
    flight = {}

    def rows_of(rel, who, length, first=0):
        return pl.ds(pl.multiple_of(rel * 256 + first + who * length, 16), length)

    def lanes_of(q):
        return pl.ds(pl.multiple_of((q % 2) * 128, 128), 128)

    def quarter_x(rel, q):
        return pl.ds(pl.multiple_of(rel * 256 + core * 128 + q * 16, 16), 16)

    def quarter_z(rel, q):
        return pl.ds(pl.multiple_of(rel * 256 + core * 128 + 64 + q * 16, 16), 16)

    def core_rows(rel, which):
        return pl.ds(pl.multiple_of(rel * 256 + which * 128, 128), 128)

    def step0(rel):
        pair_bands(rel, NC - 1)
        flight[rel] = [send(m.at[:, core_rows(rel, oc), :], r0.at[rel], G, rel * 26, other)]

    def landed(rel):
        for copy in flight[rel]:
            copy.wait_recv()
        flight[rel] = []

    def step1(rel):
        landed(rel)
        rows = core_rows(rel, core)
        m[:, rows, :] = m[:, rows, :] + r0[rel]
        for k in (1, 2, 3):
            to_x, to_z = (x + k) % 4, (z + k) % 4
            flight[rel] += [
                send(m.at[:, quarter_x(rel, to_x), :], r1.at[rel, 0, k - 1], G, rel * 26 + k, along_x[k - 1]),
                send(m.at[:, quarter_z(rel, to_z), :], r1.at[rel, 1, k - 1], G, rel * 26 + 3 + k, along_z[k - 1]),
            ]

    def step2(rel):
        landed(rel)
        for part, rows in ((0, quarter_x(rel, x)), (1, quarter_z(rel, z))):
            s[rel, part] = (m[:, rows, :] + r1[rel, part, 0]) + (r1[rel, part, 1] + r1[rel, part, 2])
        for k in (1, 2, 3):
            to_x, to_z = (x + k) % 4, (z + k) % 4
            flight[rel] += [
                send(s.at[rel, 0, to_z // 2, :, lanes_of(to_z)], r2.at[rel, 0, k - 1], G, rel * 26 + 6 + k, along_z[k - 1]),
                send(s.at[rel, 1, to_x // 2, :, lanes_of(to_x)], r2.at[rel, 1, k - 1], G, rel * 26 + 9 + k, along_x[k - 1]),
            ]

    def step3(rel):
        landed(rel)
        done = []
        for part, q, rows in ((0, z, quarter_x(rel, x)), (1, x, quarter_z(rel, z))):
            total = s[rel, part, q // 2, :, lanes_of(q)] + r2[rel, part, 0]
            total = total + (r2[rel, part, 1] + r2[rel, part, 2])
            w[q // 2, rows, lanes_of(q)] = total * wv[q // 2, :, lanes_of(q)]
            done.append(w.at[q // 2, rows, lanes_of(q)])
        for k in (1, 2, 3):
            flight[rel] += [
                send(done[0], done[0], G, rel * 26 + 12 + k, along_z[k - 1]),
                send(done[1], done[1], G, rel * 26 + 15 + k, along_x[k - 1]),
            ]

    def step4(rel):
        landed(rel)
        for_x, for_z = w.at[:, quarter_x(rel, x), :], w.at[:, quarter_z(rel, z), :]
        for k in (1, 2, 3):
            flight[rel] += [
                send(for_x, for_x, G, rel * 26 + 18 + k, along_x[k - 1]),
                send(for_z, for_z, G, rel * 26 + 21 + k, along_z[k - 1]),
            ]

    def step5(rel):
        landed(rel)
        block = w.at[:, core_rows(rel, core), :]
        flight[rel] = [send(block, block, G, rel * 26 + 25, other)]

    def step6(rel):
        landed(rel)
        left = []
        for half in (0, 1):
            plain = split(w[half, rel * 256 : rel * 256 + 256, :])
            turned = [
                jnp.concatenate([-v[64:128], v[:64], -v[192:], v[128:192]], axis=0) for v in plain
            ]
            left.append((plain, turned))

        def body(part, _):
            total = None
            for half in (0, 1):
                for imag in (0, 1):
                    rows = pl.ds(pl.multiple_of(imag * HALF + part * 512, 512), 512)
                    term = three(nt, left[half][imag], (p_hi[half, rows, :], p_lo[half, rows, :]))
                    total = term if total is None else total + term
            c[rel, 0, part] = total[:COLS]
            c[rel, 1, part] = total[COLS:]
            return 0

        lax.fori_loop(0, 2, body, 0)

    C = (c_s, c_r)
    relay = {}
    final = {}

    def step7(rel):
        if rel == 0:
            for i, part in enumerate((p, o)):
                relay[0, i] = send(c.at[0, part, 0], rl.at[0, i], C, i, up)
                relay[1, i] = send(c.at[0, part, 1], rl.at[1, i], C, 2 + i, down)
        if rel == 2:
            for i, part in enumerate((p, o)):
                for way, source, to in ((0, 1, up), (1, 2, down)):
                    free, held = 1 - way, way
                    final[way, i, free] = send(
                        c.at[source, part, free], fin.at[way, i, free], C, 4 + way * 4 + i * 2 + free, to
                    )
                for way, source, to in ((0, 1, up), (1, 2, down)):
                    held = way
                    relay[way, i].wait_recv()
                    c[source, part, held] = c[source, part, held] + rl[way, i]
                    final[way, i, held] = send(
                        c.at[source, part, held], fin.at[way, i, held], C, 4 + way * 4 + i * 2 + held, to
                    )

    steps = (step0, step1, step2, step3, step4, step5, step6, step7)
    for t in range(len(steps) + 3):
        for rel in range(4):
            if 0 <= t - rel < len(steps):
                steps[t - rel](rel)

    across = []
    for l in (0, 1):
        final[0, 0, l].wait_recv()
        final[1, 0, l].wait_recv()
        c[3, p, l] = c[3, p, l] + (fin[0, 0, l] + fin[1, 0, l])
        across.append(send(c.at[3, p, l], zin.at[l], C, 12 + l, pair))
    for l in (0, 1):
        final[0, 1, l].wait_recv()
        final[1, 1, l].wait_recv()
        lanes = pl.ds(pl.multiple_of(o * HALF + l * 512, 512), 512)
        out[:, lanes] = at[:, lanes] - (c[3, o, l] + (fin[0, 1, l] + fin[1, 1, l]))
    for l in (0, 1):
        across[l].wait_recv()
        lanes = pl.ds(pl.multiple_of(p * HALF + l * 512, 512), 512)
        out[:, lanes] = at[:, lanes] - zin[l]

    for copy in sent:
        copy.wait_send()


def projected(at, psi, wt):
    dma = pltpu.SemaphoreType.DMA
    vmem = pl.BlockSpec(memory_space=pltpu.VMEM)
    return pl.pallas_call(
        kernel,
        out_shape=jax.ShapeDtypeStruct((COLS, SLAB), F32),
        in_specs=[vmem, pl.BlockSpec(memory_space=pl.ANY), vmem],
        out_specs=vmem,
        scratch_shapes=[
            pltpu.VMEM((2, HALF, BANDS), F32),
            pltpu.VMEM((2, HALF, BANDS), F32),
            pltpu.VMEM((4, 2, COLS, HALF), F32),
            pltpu.VMEM((1024, 2 * HALF), BF16),
            pltpu.VMEM((1024, 2 * HALF), BF16),
            pltpu.VMEM((2, 2 * HALF, BANDS), BF16),
            pltpu.VMEM((2, 2 * HALF, BANDS), BF16),
            pltpu.VMEM((2, 16, BANDS), F32),
            pltpu.VMEM((2, 1024, BANDS), F32),
            pltpu.VMEM((2, 1024, BANDS), F32),
            pltpu.VMEM((4, 2, 2, COLS, 512), F32),
            pltpu.VMEM((4, 2, 128, BANDS), F32),
            pltpu.VMEM((4, 2, 3, 2, 16, BANDS), F32),
            pltpu.VMEM((4, 2, 3, 16, 128), F32),
            pltpu.VMEM((4, 2, 2, 16, BANDS), F32),
            pltpu.VMEM((2, 2, COLS, 512), F32),
            pltpu.VMEM((2, 2, 2, COLS, 512), F32),
            pltpu.VMEM((2, COLS, 512), F32),
            dma, dma((8,)), dma((8,)), dma((NC,)), dma((NC,)),
            dma((104,)), dma((104,)), dma((14,)), dma((14,)),
        ],
        compiler_params=pltpu.CompilerParams(
            collective_id=0, has_side_effects=True, vmem_limit_bytes=52 * 1024 * 1024
        ),
    )(at, psi, wt)


def per_device(psi, dpsi, band_weight, panel_band, slab_offset):
    offset = slab_offset[lax.axis_index("ga")]
    aligned = jnp.roll(jnp.swapaxes(dpsi, 1, 2), -offset, axis=2).reshape(COLS, SLAB)
    table = band_weight.reshape(-1, PANEL)
    chosen = panel_band[:, None] == jnp.arange(table.shape[0], dtype=jnp.int32)[None, :]
    weight = jnp.sum(jnp.where(chosen[:, :, None], table[None], 0.0), axis=1).reshape(1, BANDS)
    result = projected(aligned, psi, jnp.broadcast_to(weight, (16, BANDS)))
    return jnp.swapaxes(jnp.roll(result.reshape(2, COLS // 2, SLAB), offset, axis=2), 1, 2)


def solution(mesh):
    in_specs = (P(None, "ga", "ba"), P(None, "ga", "ba"), P(), P("ba"), P())
    out_specs = P(None, "ga", "ba")
    return jax.shard_map(
        per_device, mesh=mesh, in_specs=in_specs, out_specs=out_specs, check_vma=False
    )
```

profile of v0, /device:TPU:0, one launch (start us, length us, event | category | flops | bytes accessed | tf_op | source)
XLA Modules:
  0.0 135.4 jit_solution(88979927668258111)
XLA Ops:
  0.0 1.2 dynamic_slice.6
  3.9 0.7 iota_compare_fusion
  4.6 0.8 select_reduce_fusion
  5.4 2.9 %fusion.2 = f32[2,64,2048]{2,1,0:T(8,128)} fusion(s32[]{:T(128)S(6)} %select_n.22, f32[2,64,2048]{2,1,0:T(8,128)} %bitcast.10), kind=kLoop, calls=%fused_computation.6 | loop fusion | flops 262144 | bytes 2097156 | tf_op jit(solution)/shard_map/jit(_roll_dynamic)/concatenate | solution.py:365
  8.3 125.5 %shard_map.55 = f32[128,2048]{1,0:T(8,128)S(1)} custom-call(f32[128,2048]{1,0:T(8,128)} %bitcast.9, f32[2,2048,256]{2,1,0:T(8,128)} %psi.1, f32[16,256]{1,0:T(8,128)S(1)} %broadcast_in_dim.37.wt), custom_call_target="tpu_custom_call" | custom-call | tf_op jit(solution)/shard_map/pallas_call | solution.py:330
  133.8 1.6 %fusion.1 = f32[2,2048,64]{1,2,0:T(8,128)} fusion(s32[]{:T(128)S(6)} %select_n.24, f32[2,64,2048]{2,1,0:T(8,128)S(1)} %bitcast.8), kind=kLoop, calls=%fused_computation.5 | loop fusion | flops 262144 | bytes 2097156 | tf_op jit(solution)/shard_map/transpose | solution.py:370
  (1 shorter events, 0.0 us)
where the time goes:
time: 136 us; the launch traced here: 135 us
  Pallas kernels  126 us (93%)
  other arithmetic  5.98 us (4%)
  between operations  2.64 us (2%)
    pallas_call x1, Pallas kernels, projected(): pl.pallas_call(kernel, out_shape=jax.ShapeDtypeStruct((COLS, SLAB), F32),...  126 us
    concatenate x1, other arithmetic, per_device(): jnp.roll(jnp.swapaxes(dpsi, 1, 2), -offset, axis=2).reshape(COLS, SLAB)  2.88 us

commit v1 on v0

v1 whole, which is shorter than its diff:
```python
import jax
import jax.numpy as jnp
from jax import lax
from jax.experimental import pallas as pl
from jax.experimental.pallas import tpu as pltpu
from jax.sharding import PartitionSpec as P

F32, BF16 = jnp.float32, jnp.bfloat16
PANEL = 128
SLAB = 2048
BANDS = 256
COLS = 128
HALF = 768
BOTH = SLAB - 2 * HALF
MINE = HALF + BOTH
PIECES = (0, 64, 256, 512, 640, HALF)
LAST = PIECES[-2]
L2, L1 = HALF // 2, BOTH // 2
NT = (((1,), (1,)), ((), ()))


def split(value):
    high = value.astype(BF16)
    return high, (value - high.astype(F32)).astype(BF16)


def three(dot, left, right):
    return dot(left[0], right[0]) + (dot(left[0], right[1]) + dot(left[1], right[0]))


def nn(left, right):
    return jnp.dot(left, right, preferred_element_type=F32)


def nt(left, right):
    return lax.dot_general(left, right, NT, preferred_element_type=F32)


def kernel(
    raw_hbm, psi, table, panels, offsets, out,
    raw, at, psi_o, psi_p, a_v, a_hi, a_lo, o_hi, o_lo, p_hi, p_lo, ws, wv, m, w, c2, c1,
    r0, r1, r2, s, rl2, rl1, fin2, fin1, zin, zg,
    local_sem, a_s, a_r, p_s, p_r, g_s, g_r, c_s, c_r,
):
    ga, ba = lax.axis_index("ga"), lax.axis_index("ba")
    x, zhi, core = ga // 4, (ga // 2) % 2, ga % 2
    y, o = ba // 2, ba % 2
    p = 1 - o
    z = zhi * 2 + o
    oc = 1 - core

    def device(x=x, z=z, y=y, core=core):
        return (x * 4 + (z // 2) * 2 + core, y * 2 + z % 2)

    pair = device(z=zhi * 2 + p)
    up, down = device(y=(y + 1) % 4), device(y=(y + 3) % 4)
    other = device(core=oc)
    along_x = [device(x=(x + k) % 4) for k in (1, 2, 3)]
    along_z = [device(z=(z + k) % 4) for k in (1, 2, 3)]

    sent = []

    def send(src, dst, sems, index, to):
        copy = pltpu.make_async_remote_copy(
            src_ref=src, dst_ref=dst, send_sem=sems[0].at[index], recv_sem=sems[1].at[index],
            device_id=to, device_id_type=pl.DeviceIdType.MESH,
        )
        copy.start()
        sent.append(copy)
        return copy

    def half_at(which):
        return pl.multiple_of(which * HALF, HALF)

    barrier = pltpu.get_barrier_semaphore()
    peers = [up, down, other, *along_x, *along_z]
    for peer in peers:
        pl.semaphore_signal(barrier, inc=1, device_id=peer, device_id_type=pl.DeviceIdType.MESH)

    local = [
        pltpu.make_async_copy(raw_hbm, raw, local_sem.at[0]),
        pltpu.make_async_copy(
            psi.at[:, pl.ds(half_at(o), HALF), :], psi_o.at[:, pl.ds(0, HALF), :], local_sem.at[1]
        ),
        pltpu.make_async_copy(
            psi.at[:, pl.ds(2 * HALF, BOTH), :], psi_o.at[:, pl.ds(HALF, BOTH), :], local_sem.at[2]
        ),
    ]
    for copy in local:
        copy.start()

    waves = []

    def send_waves(k):
        first, count = PIECES[k], PIECES[k + 1] - PIECES[k]
        waves.append(
            send(
                psi.at[:, pl.ds(pl.multiple_of(p * HALF + first, 64), count), :],
                psi_p.at[:, pl.ds(first, count), :], (p_s, p_r), k, pair,
            )
        )

    local[0].wait()

    offset = offsets[ga]
    lane = lax.broadcasted_iota(jnp.int32, (16, 128), 1)

    def align(k, _):
        rows = pl.ds(pl.multiple_of(k * 16, 16), 16)
        tiles = [raw[rows, t * 128 : (t + 1) * 128] for t in range(16)]
        for bit in (10, 9, 8, 7, 6, 5, 4, 3, 2, 1, 0):
            turn = jnp.full((16, 128), (offset >> bit) & 1, jnp.int32) != 0
            if bit >= 7:
                moved = [tiles[(t + (1 << (bit - 7))) % 16] for t in range(16)]
            else:
                rolled = [pltpu.roll(tile, 128 - (1 << bit), 1) for tile in tiles]
                inside = lane < 128 - (1 << bit)
                moved = [jnp.where(inside, rolled[t], rolled[(t + 1) % 16]) for t in range(16)]
            tiles = [jnp.where(turn, new, old) for new, old in zip(moved, tiles)]
        for t, value in enumerate(tiles):
            if t * 128 < 2 * HALF:
                half, first = divmod(t * 128, HALF)
                at[half, rows, first : first + 128] = value
            else:
                first = t * 128 - HALF
                at[0, rows, first : first + 128] = value
                at[1, rows, first : first + 128] = value
        return 0

    lax.fori_loop(0, COLS // 16, align, 0)

    row = lax.broadcasted_iota(jnp.int32, (16, PANEL), 0)
    for k in (0, 1):
        chosen = jnp.where(row == jnp.full((16, PANEL), panels[k], jnp.int32), table[...], 0.0)
        ws[:, k * PANEL : (k + 1) * PANEL] = jnp.broadcast_to(
            jnp.sum(chosen, axis=0, keepdims=True), (16, PANEL)
        )
    wv[o] = ws[...]

    pl.semaphore_wait(barrier, len(peers))
    send_waves(0)

    A = (a_s, a_r)
    a_pair = send(at.at[p], a_v.at[3, o], A, 0, pair)
    a_up_o = send(at.at[o], a_v.at[2, o], A, 1, up)
    a_down_o = send(at.at[o], a_v.at[1, o], A, 2, down)
    w_pair = send(ws, wv.at[o], A, 7, pair)
    for k in range(1, len(PIECES) - 1):
        send_waves(k)

    def keep_columns(value, rel, half):
        rows = rel * 256 + half * COLS
        top = pl.ds(pl.multiple_of(rows, 64), 64)
        bottom = pl.ds(pl.multiple_of(rows + 64, 64), 64)
        for ref, part in zip((a_hi, a_lo), split(value)):
            ref[top, :MINE] = part[:64]
            ref[bottom, :MINE] = part[64:]
            ref[top, MINE:] = part[64:]
            ref[bottom, MINE:] = -part[:64]

    def keep_waves(ref, high_ref, low_ref, length, first, count):
        for part in (0, 1):
            high, low = split(ref[part, first : first + count, :])
            high_ref[part * length + first : part * length + first + count, :] = high
            low_ref[part * length + first : part * length + first + count, :] = low

    def keep_piece(k):
        waves[k].wait_recv()
        keep_waves(psi_p, p_hi, p_lo, HALF, PIECES[k], PIECES[k + 1] - PIECES[k])

    keep_columns(at[o], 3, o)
    local[1].wait()
    local[2].wait()
    keep_waves(psi_o, o_hi, o_lo, MINE, 0, MINE)
    keep_piece(0)

    a_pair.wait_recv()
    a_up_p = send(a_v.at[3, p], a_v.at[2, p], A, 3, up)
    a_down_p = send(a_v.at[3, p], a_v.at[1, p], A, 4, down)
    a_up_o.wait_recv()
    far_o = send(a_v.at[2, o], a_v.at[0, o], A, 5, up)
    keep_columns(a_v[3, p], 3, p)
    keep_columns(a_v[2, o], 2, o)
    a_down_o.wait_recv()
    keep_columns(a_v[1, o], 1, o)
    keep_piece(1)
    a_down_p.wait_recv()
    far_p = send(a_v.at[1, p], a_v.at[0, p], A, 6, down)
    keep_columns(a_v[1, p], 1, p)
    a_up_p.wait_recv()
    keep_columns(a_v[2, p], 2, p)
    keep_piece(2)
    w_pair.wait_recv()

    def own_bands(rel):
        rows = pl.ds(pl.multiple_of(rel * 256, 256), 256)
        m[o, rows, :] = three(nn, (a_hi[rows, :], a_lo[rows, :]), (o_hi[...], o_lo[...]))

    def pair_bands(rel, first, last):
        rows = pl.ds(pl.multiple_of(rel * 256, 256), 256)
        total = None
        for part in (0, 1):
            ks, rs = pl.ds(part * MINE + first, last - first), pl.ds(part * HALF + first, last - first)
            term = three(nn, (a_hi[rows, ks], a_lo[rows, ks]), (p_hi[rs, :], p_lo[rs, :]))
            total = term if total is None else total + term
        return rows, total

    def early(rel, _):
        own_bands(rel)
        rows, total = pair_bands(rel, 0, PIECES[3])
        m[p, rows, :] = total
        return 0

    lax.fori_loop(1, 4, early, 0)
    far_o.wait_recv()
    keep_columns(a_v[0, o], 0, o)
    far_p.wait_recv()
    keep_columns(a_v[0, p], 0, p)
    lax.fori_loop(0, 1, early, 0)
    keep_piece(3)

    def later(rel, _):
        rows, total = pair_bands(rel, PIECES[3], LAST)
        m[p, rows, :] = m[p, rows, :] + total
        return 0

    lax.fori_loop(0, 4, later, 0)
    keep_piece(4)

    G = (g_s, g_r)
    flight = {}

    def rows_of(rel, who, length, first=0):
        return pl.ds(pl.multiple_of(rel * 256 + first + who * length, 16), length)

    def lanes_of(q):
        return pl.ds(pl.multiple_of((q % 2) * 128, 128), 128)

    def quarter_x(rel, q):
        return pl.ds(pl.multiple_of(rel * 256 + core * 128 + q * 16, 16), 16)

    def quarter_z(rel, q):
        return pl.ds(pl.multiple_of(rel * 256 + core * 128 + 64 + q * 16, 16), 16)

    def core_rows(rel, which):
        return pl.ds(pl.multiple_of(rel * 256 + which * 128, 128), 128)

    def step0(rel):
        rows, total = pair_bands(rel, LAST, HALF)
        m[p, rows, :] = m[p, rows, :] + total
        flight[rel] = [send(m.at[:, core_rows(rel, oc), :], r0.at[rel], G, rel * 26, other)]

    def landed(rel):
        for copy in flight[rel]:
            copy.wait_recv()
        flight[rel] = []

    def step1(rel):
        landed(rel)
        rows = core_rows(rel, core)
        m[:, rows, :] = m[:, rows, :] + r0[rel]
        for k in (1, 2, 3):
            to_x, to_z = (x + k) % 4, (z + k) % 4
            flight[rel] += [
                send(m.at[:, quarter_x(rel, to_x), :], r1.at[rel, 0, k - 1], G, rel * 26 + k, along_x[k - 1]),
                send(m.at[:, quarter_z(rel, to_z), :], r1.at[rel, 1, k - 1], G, rel * 26 + 3 + k, along_z[k - 1]),
            ]

    def step2(rel):
        landed(rel)
        for part, rows in ((0, quarter_x(rel, x)), (1, quarter_z(rel, z))):
            s[rel, part] = (m[:, rows, :] + r1[rel, part, 0]) + (r1[rel, part, 1] + r1[rel, part, 2])
        for k in (1, 2, 3):
            to_x, to_z = (x + k) % 4, (z + k) % 4
            flight[rel] += [
                send(s.at[rel, 0, to_z // 2, :, lanes_of(to_z)], r2.at[rel, 0, k - 1], G, rel * 26 + 6 + k, along_z[k - 1]),
                send(s.at[rel, 1, to_x // 2, :, lanes_of(to_x)], r2.at[rel, 1, k - 1], G, rel * 26 + 9 + k, along_x[k - 1]),
            ]

    def step3(rel):
        landed(rel)
        done = []
        for part, q, rows in ((0, z, quarter_x(rel, x)), (1, x, quarter_z(rel, z))):
            total = s[rel, part, q // 2, :, lanes_of(q)] + r2[rel, part, 0]
            total = total + (r2[rel, part, 1] + r2[rel, part, 2])
            w[q // 2, rows, lanes_of(q)] = total * wv[q // 2, :, lanes_of(q)]
            done.append(w.at[q // 2, rows, lanes_of(q)])
        for k in (1, 2, 3):
            flight[rel] += [
                send(done[0], done[0], G, rel * 26 + 12 + k, along_z[k - 1]),
                send(done[1], done[1], G, rel * 26 + 15 + k, along_x[k - 1]),
            ]

    def step4(rel):
        landed(rel)
        for_x, for_z = w.at[:, quarter_x(rel, x), :], w.at[:, quarter_z(rel, z), :]
        for k in (1, 2, 3):
            flight[rel] += [
                send(for_x, for_x, G, rel * 26 + 18 + k, along_x[k - 1]),
                send(for_z, for_z, G, rel * 26 + 21 + k, along_z[k - 1]),
            ]

    def step5(rel):
        landed(rel)
        block = w.at[:, core_rows(rel, core), :]
        flight[rel] = [send(block, block, G, rel * 26 + 25, other)]

    C = (c_s, c_r)
    pairs = {}

    def step6(rel):
        landed(rel)
        left = []
        for half in (o, p):
            plain = split(w[half, rel * 256 : rel * 256 + 256, :])
            left.append((plain, [
                jnp.concatenate([-v[64:128], v[:64], -v[192:], v[128:192]], axis=0) for v in plain
            ]))
        mine, theirs = left

        def both(l, _):
            total = None
            for imag in (0, 1):
                rows = pl.ds(pl.multiple_of(imag * MINE + HALF + l * L1, L1), L1)
                term = three(nt, mine[imag], (o_hi[rows, :], o_lo[rows, :]))
                total = term if total is None else total + term
            c1[rel, 0, l] = total[:COLS]
            c1[rel, 1, l] = total[COLS:]
            return 0

        lax.fori_loop(0, 2, both, 0)
        pairs[rel] = send(c1.at[rel, p], zg.at[rel], C, 20 + rel, pair)

        def alone(l, _):
            total = None
            for imag in (0, 1):
                rows = pl.ds(pl.multiple_of(imag * MINE + l * L2, 128), L2)
                term = three(nt, mine[imag], (o_hi[rows, :], o_lo[rows, :]))
                total = term if total is None else total + term
                rows = pl.ds(pl.multiple_of(imag * HALF + l * L2, L2), L2)
                total = total + three(nt, theirs[imag], (p_hi[rows, :], p_lo[rows, :]))
            c2[rel, 0, l] = total[:COLS]
            c2[rel, 1, l] = total[COLS:]
            return 0

        lax.fori_loop(0, 2, alone, 0)

    ways = ((0, 1, up), (1, 2, down))
    relay, final = {}, {}

    def piece(rel, i, l):
        return (c2.at[rel, p, l], c2.at[rel, o, l], c1.at[rel, o, l])[i]

    def summed_over_pair(rel):
        pairs[rel].wait_recv()
        c1[rel, o] = c1[rel, o] + zg[rel]

    def relay_slot(way, i):
        return rl1.at[way] if i == 2 else rl2.at[way, i]

    def final_slot(way, i, l):
        return fin1.at[way, l] if i == 2 else fin2.at[way, i, l]

    def send_final(way, i, l):
        _, rel, to = ways[way]
        final[way, i, l] = send(
            piece(rel, i, l), final_slot(way, i, l), C, 6 + way * 6 + i * 2 + l, to
        )

    def step7(rel):
        if rel == 0:
            for i in (0, 1, 2):
                if i == 2:
                    summed_over_pair(0)
                for way, _, to in ways:
                    relay[way, i] = send(piece(0, i, way), relay_slot(way, i), C, way * 3 + i, to)
        if rel == 1:
            send_final(0, 0, 1)
        if rel == 2:
            send_final(1, 0, 0)
            for i in (0, 1, 2):
                for way, source, _ in ways:
                    if i == 2:
                        summed_over_pair(source)
                    if i > 0:
                        send_final(way, i, 1 - way)
                for way, source, _ in ways:
                    relay[way, i].wait_recv()
                    held = piece(source, i, way)
                    held[...] = held[...] + relay_slot(way, i)[...]
                    send_final(way, i, way)

    steps = (step0, step1, step2, step3, step4, step5, step6, step7)
    for t in range(len(steps) + 3):
        for rel in range(4):
            if 0 <= t - rel < len(steps):
                steps[t - rel](rel)

    def arrived(i, l):
        final[0, i, l].wait_recv()
        final[1, i, l].wait_recv()
        return piece(3, i, l)[...] + (final_slot(0, i, l)[...] + final_slot(1, i, l)[...])

    across = []
    for l in (0, 1):
        c2[3, p, l] = arrived(0, l)
        across.append(send(c2.at[3, p, l], zin.at[l], C, 18 + l, pair))
    for l in (0, 1):
        lanes = pl.ds(pl.multiple_of(o * HALF + l * L2, 128), L2)
        out[:, lanes] = at[o, :, l * L2 : (l + 1) * L2] - arrived(1, l)
    summed_over_pair(3)
    for l in (0, 1):
        first = HALF + l * L1
        out[:, HALF + first : HALF + first + L1] = at[o, :, first : first + L1] - arrived(2, l)
    for l in (0, 1):
        across[l].wait_recv()
        lanes = pl.ds(pl.multiple_of(p * HALF + l * L2, 128), L2)
        out[:, lanes] = at[p, :, l * L2 : (l + 1) * L2] - zin[l]

    for copy in sent:
        copy.wait_send()


def projected(raw, psi, table, panels, offsets):
    dma = pltpu.SemaphoreType.DMA
    vmem, smem = pl.BlockSpec(memory_space=pltpu.VMEM), pl.BlockSpec(memory_space=pltpu.SMEM)
    anywhere = pl.BlockSpec(memory_space=pl.ANY)
    return pl.pallas_call(
        kernel,
        out_shape=jax.ShapeDtypeStruct((COLS, SLAB), F32),
        in_specs=[anywhere, anywhere, vmem, smem, smem],
        out_specs=vmem,
        scratch_shapes=[
            pltpu.VMEM((COLS, SLAB), F32),
            pltpu.VMEM((2, COLS, MINE), F32),
            pltpu.VMEM((2, MINE, BANDS), F32),
            pltpu.VMEM((2, HALF, BANDS), F32),
            pltpu.VMEM((4, 2, COLS, MINE), F32),
            pltpu.VMEM((1024, 2 * MINE), BF16),
            pltpu.VMEM((1024, 2 * MINE), BF16),
            pltpu.VMEM((2 * MINE, BANDS), BF16),
            pltpu.VMEM((2 * MINE, BANDS), BF16),
            pltpu.VMEM((2 * HALF, BANDS), BF16),
            pltpu.VMEM((2 * HALF, BANDS), BF16),
            pltpu.VMEM((16, BANDS), F32),
            pltpu.VMEM((2, 16, BANDS), F32),
            pltpu.VMEM((2, 1024, BANDS), F32),
            pltpu.VMEM((2, 1024, BANDS), F32),
            pltpu.VMEM((4, 2, 2, COLS, L2), F32),
            pltpu.VMEM((4, 2, 2, COLS, L1), F32),
            pltpu.VMEM((4, 2, 128, BANDS), F32),
            pltpu.VMEM((4, 2, 3, 2, 16, BANDS), F32),
            pltpu.VMEM((4, 2, 3, 16, 128), F32),
            pltpu.VMEM((4, 2, 2, 16, BANDS), F32),
            pltpu.VMEM((2, 2, COLS, L2), F32),
            pltpu.VMEM((2, COLS, L1), F32),
            pltpu.VMEM((2, 2, 2, COLS, L2), F32),
            pltpu.VMEM((2, 2, COLS, L1), F32),
            pltpu.VMEM((2, COLS, L2), F32),
            pltpu.VMEM((4, 2, COLS, L1), F32),
            dma((3,)), dma((8,)), dma((8,)), dma((5,)), dma((5,)),
            dma((104,)), dma((104,)), dma((24,)), dma((24,)),
        ],
        compiler_params=pltpu.CompilerParams(
            collective_id=0, has_side_effects=True, vmem_limit_bytes=56 * 1024 * 1024
        ),
    )(raw, psi, table, panels, offsets)


def per_device(psi, dpsi, band_weight, panel_band, slab_offset):
    raw = jnp.swapaxes(dpsi, 1, 2).reshape(COLS, SLAB)
    result = projected(raw, psi, band_weight.reshape(-1, PANEL), panel_band, slab_offset)
    offset = slab_offset[lax.axis_index("ga")]
    return jnp.swapaxes(jnp.roll(result.reshape(2, COLS // 2, SLAB), offset, axis=2), 1, 2)


def solution(mesh):
    in_specs = (P(None, "ga", "ba"), P(None, "ga", "ba"), P(), P("ba"), P())
    out_specs = P(None, "ga", "ba")
    return jax.shard_map(
        per_device, mesh=mesh, in_specs=in_specs, out_specs=out_specs, check_vma=False
    )
```

time: 136 us -> 131 us (0.963)
  other arithmetic: 5.98 us -> 2.82 us
    concatenate x1 -> x0, other arithmetic: 2.88 us -> none  [per_device(): jnp.roll(jnp.swapaxes(dpsi, 1, 2), -offset, axis=2).reshape(COLS, SLAB)]
where the time goes in v1:
time: 131 us
  Pallas kernels  125 us (95%)
  other arithmetic  2.82 us (2%)
  between operations  1.97 us (2%)
    pallas_call x1, Pallas kernels, projected(): pl.pallas_call(kernel, out_shape=jax.ShapeDtypeStruct((COLS, SLAB), F32),...  125 us
    transpose x1, other arithmetic, per_device(): jnp.swapaxes(jnp.roll(result.reshape(2, COLS // 2, SLAB), offset, axis=2)...  2.82 us

profile of v1, /device:TPU:0, one launch (start us, length us, event | category | flops | bytes accessed | tf_op | source)
XLA Modules:
  0.0 130.9 jit_solution(11359308730229109320)
XLA Ops:
  0.0 1.2 dynamic_slice.7
  3.2 124.8 %shard_map.55 = f32[128,2048]{1,0:T(8,128)} custom-call(f32[128,2048]{1,0:T(8,128)} %bitcast.9, f32[2,2048,256]{2,1,0:T(8,128)} %psi.1, f32[16,128]{1,0:T(8,128)} %bitcast.10, s32[2]{0:T(128)} %panels.1, s32[16]{0:T(128)} %offsets.1), custom_call_target="tpu_custom_call" | custom-call | tf_op jit(solution)/shard_map/pallas_call | solution.py:428
  128.0 2.8 %fusion.1 = f32[2,2048,64]{1,2,0:T(8,128)} fusion(s32[]{:T(128)S(6)} %select_n.18, f32[2,64,2048]{2,1,0:T(8,128)} %bitcast.8), kind=kLoop, calls=%fused_computation.3 | loop fusion | flops 262144 | bytes 2097156 | tf_op jit(solution)/shard_map/transpose | solution.py:474

commit v2 on v1

--- a/solution.py
+++ b/solution.py
@@ -37,8 +37,8 @@
 
 
 def kernel(
-    raw_hbm, psi, table, panels, offsets, out,
-    raw, at, psi_o, psi_p, a_v, a_hi, a_lo, o_hi, o_lo, p_hi, p_lo, ws, wv, m, w, c2, c1,
+    raw_hbm, psi, table_hbm, panels_hbm, offsets_hbm, out,
+    raw, table, panels, offsets, at, psi_o, psi_p, a_v, a_hi, a_lo, o_hi, o_lo, p_hi, p_lo, ws, wv, m, w, c2, c1,
     r0, r1, r2, s, rl2, rl1, fin2, fin1, zin, zg,
     local_sem, a_s, a_r, p_s, p_r, g_s, g_r, c_s, c_r,
 ):
@@ -77,6 +77,11 @@
     for peer in peers:
         pl.semaphore_signal(barrier, inc=1, device_id=peer, device_id_type=pl.DeviceIdType.MESH)
 
+    small = [
+        pltpu.make_async_copy(offsets_hbm, offsets, local_sem.at[3]),
+        pltpu.make_async_copy(table_hbm, table, local_sem.at[4]),
+        pltpu.make_async_copy(panels_hbm, panels, local_sem.at[5]),
+    ]
     local = [
         pltpu.make_async_copy(raw_hbm, raw, local_sem.at[0]),
         pltpu.make_async_copy(
@@ -86,7 +91,7 @@
             psi.at[:, pl.ds(2 * HALF, BOTH), :], psi_o.at[:, pl.ds(HALF, BOTH), :], local_sem.at[2]
         ),
     ]
-    for copy in local:
+    for copy in small + local:
         copy.start()
 
     waves = []
@@ -100,6 +105,10 @@
             )
         )
 
+    pl.semaphore_wait(barrier, len(peers))
+    send_waves(0)
+    for copy in small:
+        copy.wait()
     local[0].wait()
 
     offset = offsets[ga]
@@ -137,9 +146,6 @@
         )
     wv[o] = ws[...]
 
-    pl.semaphore_wait(barrier, len(peers))
-    send_waves(0)
-
     A = (a_s, a_r)
     a_pair = send(at.at[p], a_v.at[3, o], A, 0, pair)
     a_up_o = send(at.at[o], a_v.at[2, o], A, 1, up)
@@ -196,8 +202,10 @@
         rows = pl.ds(pl.multiple_of(rel * 256, 256), 256)
         m[o, rows, :] = three(nn, (a_hi[rows, :], a_lo[rows, :]), (o_hi[...], o_lo[...]))
 
-    def pair_bands(rel, first, last):
-        rows = pl.ds(pl.multiple_of(rel * 256, 256), 256)
+    def block_rows(rel):
+        return pl.ds(pl.multiple_of(rel * 256, 256), 256)
+
+    def pair_bands(rows, first, last):
         total = None
         for part in (0, 1):
             ks, rs = pl.ds(part * MINE + first, last - first), pl.ds(part * HALF + first, last - first)
@@ -207,7 +215,7 @@
 
     def early(rel, _):
         own_bands(rel)
-        rows, total = pair_bands(rel, 0, PIECES[3])
+        rows, total = pair_bands(block_rows(rel), 0, PIECES[3])
         m[p, rows, :] = total
         return 0
 
@@ -220,7 +228,7 @@
     keep_piece(3)
 
     def later(rel, _):
-        rows, total = pair_bands(rel, PIECES[3], LAST)
+        rows, total = pair_bands(block_rows(rel), PIECES[3], LAST)
         m[p, rows, :] = m[p, rows, :] + total
         return 0
 
@@ -228,122 +236,115 @@
     keep_piece(4)
 
     G = (g_s, g_r)
+    chunks = ((0, 128), (128, 128), (256, 256), (512, 256), (768, 256))
     flight = {}
 
-    def rows_of(rel, who, length, first=0):
-        return pl.ds(pl.multiple_of(rel * 256 + first + who * length, 16), length)
-
-    def lanes_of(q):
-        return pl.ds(pl.multiple_of((q % 2) * 128, 128), 128)
-
-    def quarter_x(rel, q):
-        return pl.ds(pl.multiple_of(rel * 256 + core * 128 + q * 16, 16), 16)
-
-    def quarter_z(rel, q):
-        return pl.ds(pl.multiple_of(rel * 256 + core * 128 + 64 + q * 16, 16), 16)
-
-    def core_rows(rel, which):
-        return pl.ds(pl.multiple_of(rel * 256 + which * 128, 128), 128)
-
-    def step0(rel):
-        rows, total = pair_bands(rel, LAST, HALF)
+    def quarter(n, part, q):
+        first, length = chunks[n]
+        return pl.ds(
+            pl.multiple_of(first + (core * 2 + part) * (length // 4) + q * (length // 16), 8),
+            length // 16,
+        )
+
+    def core_rows(n, which):
+        first, length = chunks[n]
+        return pl.ds(pl.multiple_of(first + which * (length // 2), 64), length // 2)
+
+    def landed(n):
+        for copy in flight[n]:
+            copy.wait_recv()
+        flight[n] = []
+
+    def step0(n):
+        first, length = chunks[n]
+        rows, total = pair_bands(pl.ds(first, length), LAST, HALF)
         m[p, rows, :] = m[p, rows, :] + total
-        flight[rel] = [send(m.at[:, core_rows(rel, oc), :], r0.at[rel], G, rel * 26, other)]
-
-    def landed(rel):
-        for copy in flight[rel]:
-            copy.wait_recv()
-        flight[rel] = []
-
-    def step1(rel):
-        landed(rel)
-        rows = core_rows(rel, core)
-        m[:, rows, :] = m[:, rows, :] + r0[rel]
+        to = r0.at[:, pl.ds(first // 2, length // 2), :]
+        flight[n] = [send(m.at[:, core_rows(n, oc), :], to, G, n * 20, other)]
+
+    def step1(n):
+        landed(n)
+        first, length = chunks[n]
+        rows = core_rows(n, core)
+        m[:, rows, :] = m[:, rows, :] + r0[:, first // 2 : (first + length) // 2, :]
+        few = pl.ds(0, length // 16)
         for k in (1, 2, 3):
             to_x, to_z = (x + k) % 4, (z + k) % 4
-            flight[rel] += [
-                send(m.at[:, quarter_x(rel, to_x), :], r1.at[rel, 0, k - 1], G, rel * 26 + k, along_x[k - 1]),
-                send(m.at[:, quarter_z(rel, to_z), :], r1.at[rel, 1, k - 1], G, rel * 26 + 3 + k, along_z[k - 1]),
+            flight[n] += [
+                send(m.at[:, quarter(n, 0, to_x), :], r1.at[n, 0, k - 1, :, few], G, n * 20 + k, along_x[k - 1]),
+                send(m.at[:, quarter(n, 1, to_z), :], r1.at[n, 1, k - 1, :, few], G, n * 20 + 3 + k, along_z[k - 1]),
             ]
 
-    def step2(rel):
-        landed(rel)
-        for part, rows in ((0, quarter_x(rel, x)), (1, quarter_z(rel, z))):
-            s[rel, part] = (m[:, rows, :] + r1[rel, part, 0]) + (r1[rel, part, 1] + r1[rel, part, 2])
+    def four(mine, ref, n, part):
+        few = chunks[n][1] // 16
+        return (mine + ref[n, part, 0, :, :few]) + (ref[n, part, 1, :, :few] + ref[n, part, 2, :, :few])
+
+    def step2(n):
+        landed(n)
+        few = pl.ds(0, chunks[n][1] // 16)
+        for part, q in ((0, x), (1, z)):
+            s[n, part, :, few, :] = four(m[:, quarter(n, part, q), :], r1, n, part)
         for k in (1, 2, 3):
-            to_x, to_z = (x + k) % 4, (z + k) % 4
-            flight[rel] += [
-                send(s.at[rel, 0, to_z // 2, :, lanes_of(to_z)], r2.at[rel, 0, k - 1], G, rel * 26 + 6 + k, along_z[k - 1]),
-                send(s.at[rel, 1, to_x // 2, :, lanes_of(to_x)], r2.at[rel, 1, k - 1], G, rel * 26 + 9 + k, along_x[k - 1]),
+            flight[n] += [
+                send(s.at[n, 0, :, few], r2.at[n, 0, k - 1, :, few], G, n * 20 + 6 + k, along_z[k - 1]),
+                send(s.at[n, 1, :, few], r2.at[n, 1, k - 1, :, few], G, n * 20 + 9 + k, along_x[k - 1]),
             ]
 
-    def step3(rel):
-        landed(rel)
-        done = []
-        for part, q, rows in ((0, z, quarter_x(rel, x)), (1, x, quarter_z(rel, z))):
-            total = s[rel, part, q // 2, :, lanes_of(q)] + r2[rel, part, 0]
-            total = total + (r2[rel, part, 1] + r2[rel, part, 2])
-            w[q // 2, rows, lanes_of(q)] = total * wv[q // 2, :, lanes_of(q)]
-            done.append(w.at[q // 2, rows, lanes_of(q)])
+    def step3(n):
+        landed(n)
+        few = chunks[n][1] // 16
+        for part, q in ((0, x), (1, z)):
+            w[:, quarter(n, part, q), :] = four(s[n, part, :, :few], r2, n, part) * wv[:, :few, :]
+        for_x, for_z = w.at[:, quarter(n, 0, x), :], w.at[:, quarter(n, 1, z), :]
         for k in (1, 2, 3):
-            flight[rel] += [
-                send(done[0], done[0], G, rel * 26 + 12 + k, along_z[k - 1]),
-                send(done[1], done[1], G, rel * 26 + 15 + k, along_x[k - 1]),
+            flight[n] += [
+                send(for_x, for_x, G, n * 20 + 12 + k, along_x[k - 1]),
+                send(for_z, for_z, G, n * 20 + 15 + k, along_z[k - 1]),
             ]
 
-    def step4(rel):
-        landed(rel)
-        for_x, for_z = w.at[:, quarter_x(rel, x), :], w.at[:, quarter_z(rel, z), :]
-        for k in (1, 2, 3):
-            flight[rel] += [
-                send(for_x, for_x, G, rel * 26 + 18 + k, along_x[k - 1]),
-                send(for_z, for_z, G, rel * 26 + 21 + k, along_z[k - 1]),
-            ]
-
-    def step5(rel):
-        landed(rel)
-        block = w.at[:, core_rows(rel, core), :]
-        flight[rel] = [send(block, block, G, rel * 26 + 25, other)]
+    def step4(n):
+        landed(n)
+        block = w.at[:, core_rows(n, core), :]
+        flight[n] = [send(block, block, G, n * 20 + 19, other)]
 
     C = (c_s, c_r)
     pairs = {}
 
-    def step6(rel):
-        landed(rel)
+    def corrections(n, after=None):
+        landed(n)
+        first, length = chunks[n]
+        rel, blocks = first // 256, range(first % 256 // COLS, (first % 256 + length) // COLS)
         left = []
         for half in (o, p):
-            plain = split(w[half, rel * 256 : rel * 256 + 256, :])
-            left.append((plain, [
-                jnp.concatenate([-v[64:128], v[:64], -v[192:], v[128:192]], axis=0) for v in plain
-            ]))
+            plain = split(w[half, first : first + length, :])
+            turned = []
+            for v in plain:
+                rows = [(-v[r + 64 : r + 128], v[r : r + 64]) for r in range(0, length, COLS)]
+                turned.append(jnp.concatenate([part for two in rows for part in two], axis=0))
+            left.append((plain, turned))
         mine, theirs = left
 
-        def both(l, _):
+        def both(l):
             total = None
             for imag in (0, 1):
-                rows = pl.ds(pl.multiple_of(imag * MINE + HALF + l * L1, L1), L1)
+                rows = pl.ds(imag * MINE + HALF + l * L1, L1)
                 term = three(nt, mine[imag], (o_hi[rows, :], o_lo[rows, :]))
                 total = term if total is None else total + term
-            c1[rel, 0, l] = total[:COLS]
-            c1[rel, 1, l] = total[COLS:]
-            return 0
-
-        lax.fori_loop(0, 2, both, 0)
-        pairs[rel] = send(c1.at[rel, p], zg.at[rel], C, 20 + rel, pair)
-
-        def alone(l, _):
+            for i, block in enumerate(blocks):
+                c1[rel, block, l] = total[i * COLS : (i + 1) * COLS]
+
+        def alone(l):
             total = None
             for imag in (0, 1):
-                rows = pl.ds(pl.multiple_of(imag * MINE + l * L2, 128), L2)
+                rows = pl.ds(imag * MINE + l * L2, L2)
                 term = three(nt, mine[imag], (o_hi[rows, :], o_lo[rows, :]))
                 total = term if total is None else total + term
-                rows = pl.ds(pl.multiple_of(imag * HALF + l * L2, L2), L2)
+                rows = pl.ds(imag * HALF + l * L2, L2)
                 total = total + three(nt, theirs[imag], (p_hi[rows, :], p_lo[rows, :]))
-            c2[rel, 0, l] = total[:COLS]
-            c2[rel, 1, l] = total[COLS:]
-            return 0
-
-        lax.fori_loop(0, 2, alone, 0)
+            for i, block in enumerate(blocks):
+                c2[rel, block, l] = total[i * COLS : (i + 1) * COLS]
+
+        return both, alone
 
     ways = ((0, 1, up), (1, 2, down))
     relay, final = {}, {}
@@ -354,9 +355,6 @@
     def summed_over_pair(rel):
         pairs[rel].wait_recv()
         c1[rel, o] = c1[rel, o] + zg[rel]
-
-    def relay_slot(way, i):
-        return rl1.at[way] if i == 2 else rl2.at[way, i]
 
     def final_slot(way, i, l):
         return fin1.at[way, l] if i == 2 else fin2.at[way, i, l]
@@ -367,17 +365,35 @@
             piece(rel, i, l), final_slot(way, i, l), C, 6 + way * 6 + i * 2 + l, to
         )
 
-    def step7(rel):
-        if rel == 0:
-            for i in (0, 1, 2):
-                if i == 2:
-                    summed_over_pair(0)
-                for way, _, to in ways:
-                    relay[way, i] = send(piece(0, i, way), relay_slot(way, i), C, way * 3 + i, to)
-        if rel == 1:
+    def to_pair(rel):
+        pairs[rel] = send(c1.at[rel, p], zg.at[rel], C, 20 + rel, pair)
+
+    def step5(n):
+        both, alone = corrections(n)
+        if n < 2:
+            for way, _, to in ways:
+                alone(way)
+                relay[way, n] = send(c2.at[0, n, way], rl2.at[way, n], C, way * 3 + n, to)
+            both(0)
+            both(1)
+            if n == 1:
+                to_pair(0)
+        else:
+            both(0)
+            both(1)
+            to_pair(n - 1)
+            alone(1)
+            alone(0)
+        if n == 2:
             send_final(0, 0, 1)
-        if rel == 2:
+            summed_over_pair(0)
+            for way, _, to in ways:
+                relay[way, 2] = send(piece(0, 2, way), rl1.at[way], C, way * 3 + 2, to)
+        if n == 3:
             send_final(1, 0, 0)
+            for way in (0, 1):
+                relay[way, 0].wait_recv()
+                relay[way, 1].wait_recv()
             for i in (0, 1, 2):
                 for way, source, _ in ways:
                     if i == 2:
@@ -385,16 +401,17 @@
                     if i > 0:
                         send_final(way, i, 1 - way)
                 for way, source, _ in ways:
-                    relay[way, i].wait_recv()
+                    if i == 2:
+                        relay[way, 2].wait_recv()
                     held = piece(source, i, way)
-                    held[...] = held[...] + relay_slot(way, i)[...]
+                    held[...] = held[...] + (rl1[way] if i == 2 else rl2[way, (p, o)[i]])
                     send_final(way, i, way)
 
-    steps = (step0, step1, step2, step3, step4, step5, step6, step7)
-    for t in range(len(steps) + 3):
-        for rel in range(4):
-            if 0 <= t - rel < len(steps):
-                steps[t - rel](rel)
+    steps = (step0, step1, step2, step3, step4, step5)
+    for t in range(len(steps) + len(chunks) - 1):
+        for n in range(len(chunks)):
+            if 0 <= t - n < len(steps):
+                steps[t - n](n)
 
     def arrived(i, l):
         final[0, i, l].wait_recv()
@@ -423,15 +440,17 @@
 
 def projected(raw, psi, table, panels, offsets):
     dma = pltpu.SemaphoreType.DMA
-    vmem, smem = pl.BlockSpec(memory_space=pltpu.VMEM), pl.BlockSpec(memory_space=pltpu.SMEM)
-    anywhere = pl.BlockSpec(memory_space=pl.ANY)
+    vmem, hbm = pl.BlockSpec(memory_space=pltpu.VMEM), pl.BlockSpec(memory_space=pltpu.HBM)
     return pl.pallas_call(
         kernel,
         out_shape=jax.ShapeDtypeStruct((COLS, SLAB), F32),
-        in_specs=[anywhere, anywhere, vmem, smem, smem],
+        in_specs=[hbm] * 5,
         out_specs=vmem,
         scratch_shapes=[
             pltpu.VMEM((COLS, SLAB), F32),
+            pltpu.VMEM((16, PANEL), F32),
+            pltpu.SMEM((2,), jnp.int32),
+            pltpu.SMEM((16,), jnp.int32),
             pltpu.VMEM((2, COLS, MINE), F32),
             pltpu.VMEM((2, MINE, BANDS), F32),
             pltpu.VMEM((2, HALF, BANDS), F32),
@@ -448,30 +467,47 @@
             pltpu.VMEM((2, 1024, BANDS), F32),
             pltpu.VMEM((4, 2, 2, COLS, L2), F32),
             pltpu.VMEM((4, 2, 2, COLS, L1), F32),
-            pltpu.VMEM((4, 2, 128, BANDS), F32),
-            pltpu.VMEM((4, 2, 3, 2, 16, BANDS), F32),
-            pltpu.VMEM((4, 2, 3, 16, 128), F32),
-            pltpu.VMEM((4, 2, 2, 16, BANDS), F32),
+            pltpu.VMEM((2, 512, BANDS), F32),
+            pltpu.VMEM((5, 2, 3, 2, 16, BANDS), F32),
+            pltpu.VMEM((5, 2, 3, 2, 16, BANDS), F32),
+            pltpu.VMEM((5, 2, 2, 16, BANDS), F32),
             pltpu.VMEM((2, 2, COLS, L2), F32),
             pltpu.VMEM((2, COLS, L1), F32),
             pltpu.VMEM((2, 2, 2, COLS, L2), F32),
             pltpu.VMEM((2, 2, COLS, L1), F32),
             pltpu.VMEM((2, COLS, L2), F32),
             pltpu.VMEM((4, 2, COLS, L1), F32),
-            dma((3,)), dma((8,)), dma((8,)), dma((5,)), dma((5,)),
-            dma((104,)), dma((104,)), dma((24,)), dma((24,)),
+            dma((6,)), dma((8,)), dma((8,)), dma((5,)), dma((5,)),
+            dma((100,)), dma((100,)), dma((24,)), dma((24,)),
         ],
         compiler_params=pltpu.CompilerParams(
-            collective_id=0, has_side_effects=True, vmem_limit_bytes=56 * 1024 * 1024
+            collective_id=0, has_side_effects=True, vmem_limit_bytes=52 * 1024 * 1024
         ),
     )(raw, psi, table, panels, offsets)
+
+
+def turn_kernel(offsets, value, out):
+    offset = offsets[lax.axis_index("ga")]
+    for part in (0, 1):
+        out[part] = pltpu.roll(value[part], offset, 1)
+
+
+def turned_back(value, offsets):
+    block = pl.BlockSpec((2, 16, SLAB), lambda k: (0, k, 0))
+    return pl.pallas_call(
+        turn_kernel,
+        grid=(COLS // 2 // 16,),
+        out_shape=jax.ShapeDtypeStruct((2, COLS // 2, SLAB), F32),
+        in_specs=[pl.BlockSpec(memory_space=pltpu.SMEM), block],
+        out_specs=block,
+        compiler_params=pltpu.CompilerParams(vmem_limit_bytes=8 * 1024 * 1024),
+    )(offsets, value)
 
 
 def per_device(psi, dpsi, band_weight, panel_band, slab_offset):
     raw = jnp.swapaxes(dpsi, 1, 2).reshape(COLS, SLAB)
     result = projected(raw, psi, band_weight.reshape(-1, PANEL), panel_band, slab_offset)
-    offset = slab_offset[lax.axis_index("ga")]
-    return jnp.swapaxes(jnp.roll(result.reshape(2, COLS // 2, SLAB), offset, axis=2), 1, 2)
+    return jnp.swapaxes(turned_back(result.reshape(2, COLS // 2, SLAB), slab_offset), 1, 2)
 
 
 def solution(mesh):

time: 131 us -> 132 us (level)
  Pallas kernels: 125 us -> 129 us
  other arithmetic: 2.82 us -> 0 us
  between operations: 1.97 us -> 0.01 us
    transpose x1 -> x0, other arithmetic: 2.82 us -> none  [per_device(): jnp.swapaxes(jnp.roll(result.reshape(2, COLS // 2, SLAB), offset, axis=2)...]
    pallas_call x0 -> x1, Pallas kernels: none -> 2.52 us  [turned_back(): pl.pallas_call(turn_kernel, grid=(COLS // 2 // 16,), out_shape=jax.ShapeD...]
    unnamed x0 -> x6, local copies, waits for them, and re-layouts: none -> 2.01 us
where the time goes in v2:
time: 132 us; the launch traced here: 131 us
  Pallas kernels  129 us (98%)
  local copies, waits for them, and re-layouts  2.01 us (2%)
    pallas_call x1, Pallas kernels, projected(): pl.pallas_call(kernel, out_shape=jax.ShapeDtypeStruct((COLS, SLAB), F32),...  126 us

profile of v2, /device:TPU:0, one launch (start us, length us, event | category | flops | bytes accessed | tf_op | source)
XLA Modules:
  0.0 130.6 jit_solution(13611239299957574933)
XLA Ops:
  0.0 0.0 copy-start
  0.0 0.7 copy-done
  0.7 0.0 copy-start.1
  0.7 0.7 copy-done.1
  1.4 0.0 copy-start.2
  1.4 0.7 copy-done.2
  2.0 126.1 %shard_map.55 = f32[128,2048]{1,0:T(8,128)S(1)} custom-call(f32[128,2048]{1,0:T(8,128)} %bitcast.8, f32[2,2048,256]{2,1,0:T(8,128)} %psi.1, f32[16,128]{1,0:T(8,128)S(1)} %bitcast.7, s32[2]{0:T(128)S(1)} %copy-done.2, s32[16]{0:T(128)S(1)} %copy-done.1), custom_call_target="tpu_custom_call" | custom-call | tf_op jit(solution)/shard_map/pallas_call | solution.py:444
  128.1 2.5 %shard_map.56 = f32[2,64,2048]{2,1,0:T(8,128)} custom-call(s32[16]{0:T(128)S(1)} %copy-done.1, f32[2,64,2048]{2,1,0:T(8,128)S(1)} %bitcast.6), custom_call_target="tpu_custom_call" | custom-call | tf_op jit(solution)/shard_map/pallas_call | solution.py:497
Async XLA Ops:
  0.0 0.7 copy-start
  0.7 0.7 copy-start.1
  1.4 0.7 copy-start.2

commit v3 on v2

--- a/solution.py
+++ b/solution.py
@@ -142,15 +142,29 @@
     for k in (0, 1):
         chosen = jnp.where(row == jnp.full((16, PANEL), panels[k], jnp.int32), table[...], 0.0)
         ws[:, k * PANEL : (k + 1) * PANEL] = jnp.broadcast_to(
-            jnp.sum(chosen, axis=0, keepdims=True), (16, PANEL)
+            jnp.sum(chosen, axis=0, keepdims=True), (32, PANEL)
         )
     wv[o] = ws[...]
 
     A = (a_s, a_r)
-    a_pair = send(at.at[p], a_v.at[3, o], A, 0, pair)
-    a_up_o = send(at.at[o], a_v.at[2, o], A, 1, up)
-    a_down_o = send(at.at[o], a_v.at[1, o], A, 2, down)
-    w_pair = send(ws, wv.at[o], A, 7, pair)
+    lanes = (pl.ds(0, MINE // 2), pl.ds(MINE // 2, MINE // 2))
+    a_pair = [send(at.at[p, :, l], a_v.at[3, o, :, l], A, i, pair) for i, l in enumerate(lanes)]
+    ring = ((0, up, 2), (1, down, 1))
+
+    def pass_on(source, half, base):
+        return {
+            (way, i): send(source.at[:, lanes[i]], a_v.at[slot, half, :, lanes[i]], A, base + way * 2 + i, to)
+            for order in (0, 1) for way, to, slot in ring for i in (way ^ order,)
+        }
+
+    def forward(half, base):
+        return [
+            send(a_v.at[slot, half, :, lanes[way]], a_v.at[0, half, :, lanes[way]], A, base + way, to)
+            for way, to, slot in ring
+        ]
+
+    near_o = pass_on(at.at[o], o, 2)
+    w_pair = send(ws, wv.at[o], A, 14, pair)
     for k in range(1, len(PIECES) - 1):
         send_waves(k)
 
@@ -180,22 +194,27 @@
     keep_waves(psi_o, o_hi, o_lo, MINE, 0, MINE)
     keep_piece(0)
 
-    a_pair.wait_recv()
-    a_up_p = send(a_v.at[3, p], a_v.at[2, p], A, 3, up)
-    a_down_p = send(a_v.at[3, p], a_v.at[1, p], A, 4, down)
-    a_up_o.wait_recv()
-    far_o = send(a_v.at[2, o], a_v.at[0, o], A, 5, up)
+    for way in (0, 1):
+        near_o[way, way].wait_recv()
+    far_o = forward(o, 10)
+    a_pair[0].wait_recv()
+    a_pair[1].wait_recv()
+    near_p = pass_on(a_v.at[3, p], p, 6)
     keep_columns(a_v[3, p], 3, p)
-    keep_columns(a_v[2, o], 2, o)
-    a_down_o.wait_recv()
-    keep_columns(a_v[1, o], 1, o)
+    for way, _, slot in ring:
+        near_o[way, 1 - way].wait_recv()
+        keep_columns(a_v[slot, o], slot, o)
     keep_piece(1)
-    a_down_p.wait_recv()
-    far_p = send(a_v.at[1, p], a_v.at[0, p], A, 6, down)
-    keep_columns(a_v[1, p], 1, p)
-    a_up_p.wait_recv()
-    keep_columns(a_v[2, p], 2, p)
+    for way in (0, 1):
+        near_p[way, way].wait_recv()
+    far_p = forward(p, 12)
+    for copy in far_o:
+        copy.wait_recv()
+    keep_columns(a_v[0, o], 0, o)
     keep_piece(2)
+    for way, _, slot in ring:
+        near_p[way, 1 - way].wait_recv()
+        keep_columns(a_v[slot, p], slot, p)
     w_pair.wait_recv()
 
     def own_bands(rel):
@@ -220,9 +239,8 @@
         return 0
 
     lax.fori_loop(1, 4, early, 0)
-    far_o.wait_recv()
-    keep_columns(a_v[0, o], 0, o)
-    far_p.wait_recv()
+    for copy in far_p:
+        copy.wait_recv()
     keep_columns(a_v[0, p], 0, p)
     lax.fori_loop(0, 1, early, 0)
     keep_piece(3)
@@ -236,7 +254,7 @@
     keep_piece(4)
 
     G = (g_s, g_r)
-    chunks = ((0, 128), (128, 128), (256, 256), (512, 256), (768, 256))
+    chunks = ((0, 256), (256, 512), (768, 256))
     flight = {}
 
     def quarter(n, part, q):
@@ -310,18 +328,13 @@
     C = (c_s, c_r)
     pairs = {}
 
-    def corrections(n, after=None):
-        landed(n)
-        first, length = chunks[n]
-        rel, blocks = first // 256, range(first % 256 // COLS, (first % 256 + length) // COLS)
+    def corrections(rel):
         left = []
         for half in (o, p):
-            plain = split(w[half, first : first + length, :])
-            turned = []
-            for v in plain:
-                rows = [(-v[r + 64 : r + 128], v[r : r + 64]) for r in range(0, length, COLS)]
-                turned.append(jnp.concatenate([part for two in rows for part in two], axis=0))
-            left.append((plain, turned))
+            plain = split(w[half, rel * 256 : rel * 256 + 256, :])
+            left.append((plain, [
+                jnp.concatenate([-v[64:128], v[:64], -v[192:], v[128:192]], axis=0) for v in plain
+            ]))
         mine, theirs = left
 
         def both(l):
@@ -330,8 +343,8 @@
                 rows = pl.ds(imag * MINE + HALF + l * L1, L1)
                 term = three(nt, mine[imag], (o_hi[rows, :], o_lo[rows, :]))
                 total = term if total is None else total + term
-            for i, block in enumerate(blocks):
-                c1[rel, block, l] = total[i * COLS : (i + 1) * COLS]
+            c1[rel, 0, l] = total[:COLS]
+            c1[rel, 1, l] = total[COLS:]
 
         def alone(l):
             total = None
@@ -341,8 +354,8 @@
                 total = term if total is None else total + term
                 rows = pl.ds(imag * HALF + l * L2, L2)
                 total = total + three(nt, theirs[imag], (p_hi[rows, :], p_lo[rows, :]))
-            for i, block in enumerate(blocks):
-                c2[rel, block, l] = total[i * COLS : (i + 1) * COLS]
+            c2[rel, 0, l] = total[:COLS]
+            c2[rel, 1, l] = total[COLS:]
 
         return both, alone
 
@@ -368,44 +381,57 @@
     def to_pair(rel):
         pairs[rel] = send(c1.at[rel, p], zg.at[rel], C, 20 + rel, pair)
 
+    def send_relay(i):
+        for way, _, to in ways:
+            slot = rl1.at[way] if i == 2 else rl2.at[way, i]
+            relay[way, i] = send(piece(0, i, way), slot, C, way * 3 + i, to)
+
+    def send_held(way, i):
+        relay[way, i].wait_recv()
+        held = piece(ways[way][1], i, way)
+        held[...] = held[...] + (rl1[way] if i == 2 else rl2[way, i])
+        send_final(way, i, way)
+
     def step5(n):
-        both, alone = corrections(n)
-        if n < 2:
-            for way, _, to in ways:
-                alone(way)
-                relay[way, n] = send(c2.at[0, n, way], rl2.at[way, n], C, way * 3 + n, to)
+        landed(n)
+        if n == 0:
+            both, alone = corrections(0)
+            alone(0)
+            alone(1)
+            send_relay(0)
+            send_relay(1)
             both(0)
             both(1)
-            if n == 1:
-                to_pair(0)
+            to_pair(0)
+        elif n == 1:
+            for way, rel, _ in ways:
+                both, alone = corrections(rel)
+                both(0)
+                both(1)
+                to_pair(rel)
+                alone(1 - way)
+                send_final(way, 0, 1 - way)
+                alone(way)
+            summed_over_pair(0)
+            send_relay(2)
+            for i in (0, 1):
+                for way in (0, 1):
+                    if i > 0:
+                        send_final(way, i, 1 - way)
+                for way in (0, 1):
+                    send_held(way, i)
         else:
+            both, alone = corrections(3)
             both(0)
             both(1)
-            to_pair(n - 1)
+            to_pair(3)
+            for way, rel, _ in ways:
+                summed_over_pair(rel)
+                send_final(way, 2, 1 - way)
+            for way in (0, 1):
+                send_held(way, 2)
+            alone(0)
             alone(1)
-            alone(0)
-        if n == 2:
-            send_final(0, 0, 1)
-            summed_over_pair(0)
-            for way, _, to in ways:
-                relay[way, 2] = send(piece(0, 2, way), rl1.at[way], C, way * 3 + 2, to)
-        if n == 3:
-            send_final(1, 0, 0)
-            for way in (0, 1):
-                relay[way, 0].wait_recv()
-                relay[way, 1].wait_recv()
-            for i in (0, 1, 2):
-                for way, source, _ in ways:
-                    if i == 2:
-                        summed_over_pair(source)
-                    if i > 0:
-                        send_final(way, i, 1 - way)
-                for way, source, _ in ways:
-                    if i == 2:
-                        relay[way, 2].wait_recv()
-                    held = piece(source, i, way)
-                    held[...] = held[...] + (rl1[way] if i == 2 else rl2[way, (p, o)[i]])
-                    send_final(way, i, way)
 
     steps = (step0, step1, step2, step3, step4, step5)
     for t in range(len(steps) + len(chunks) - 1):
@@ -461,27 +487,27 @@
             pltpu.VMEM((2 * MINE, BANDS), BF16),
             pltpu.VMEM((2 * HALF, BANDS), BF16),
             pltpu.VMEM((2 * HALF, BANDS), BF16),
-            pltpu.VMEM((16, BANDS), F32),
-            pltpu.VMEM((2, 16, BANDS), F32),
+            pltpu.VMEM((32, BANDS), F32),
+            pltpu.VMEM((2, 32, BANDS), F32),
             pltpu.VMEM((2, 1024, BANDS), F32),
             pltpu.VMEM((2, 1024, BANDS), F32),
             pltpu.VMEM((4, 2, 2, COLS, L2), F32),
             pltpu.VMEM((4, 2, 2, COLS, L1), F32),
             pltpu.VMEM((2, 512, BANDS), F32),
-            pltpu.VMEM((5, 2, 3, 2, 16, BANDS), F32),
-            pltpu.VMEM((5, 2, 3, 2, 16, BANDS), F32),
-            pltpu.VMEM((5, 2, 2, 16, BANDS), F32),
+            pltpu.VMEM((3, 2, 3, 2, 32, BANDS), F32),
+            pltpu.VMEM((3, 2, 3, 2, 32, BANDS), F32),
+            pltpu.VMEM((3, 2, 2, 32, BANDS), F32),
             pltpu.VMEM((2, 2, COLS, L2), F32),
             pltpu.VMEM((2, COLS, L1), F32),
             pltpu.VMEM((2, 2, 2, COLS, L2), F32),
             pltpu.VMEM((2, 2, COLS, L1), F32),
             pltpu.VMEM((2, COLS, L2), F32),
             pltpu.VMEM((4, 2, COLS, L1), F32),
-            dma((6,)), dma((8,)), dma((8,)), dma((5,)), dma((5,)),
-            dma((100,)), dma((100,)), dma((24,)), dma((24,)),
+            dma((6,)), dma((15,)), dma((15,)), dma((5,)), dma((5,)),
+            dma((60,)), dma((60,)), dma((24,)), dma((24,)),
         ],
         compiler_params=pltpu.CompilerParams(
-            collective_id=0, has_side_effects=True, vmem_limit_bytes=52 * 1024 * 1024
+            collective_id=0, has_side_effects=True, vmem_limit_bytes=62 * 1024 * 1024
         ),
     )(raw, psi, table, panels, offsets)
 
@@ -500,7 +526,7 @@
         out_shape=jax.ShapeDtypeStruct((2, COLS // 2, SLAB), F32),
         in_specs=[pl.BlockSpec(memory_space=pltpu.SMEM), block],
         out_specs=block,
-        compiler_params=pltpu.CompilerParams(vmem_limit_bytes=8 * 1024 * 1024),
+        compiler_params=pltpu.CompilerParams(vmem_limit_bytes=62 * 1024 * 1024),
     )(offsets, value)
 
 

time: 132 us -> 122 us (0.924); the launches traced: 131 us -> 122 us
  Pallas kernels: 129 us -> 122 us
  local copies, waits for them, and re-layouts: 2.01 us -> 0 us
    pallas_call x1, Pallas kernels: 126 us -> 118 us  [projected(): pl.pallas_call(kernel, out_shape=jax.ShapeDtypeStruct((COLS, SLAB), F32),...]
    unnamed x6 -> x0, local copies, waits for them, and re-layouts: 2.01 us -> none
where the time goes in v3:
time: 122 us
  Pallas kernels  122 us (100%)
    pallas_call x1, Pallas kernels, projected(): pl.pallas_call(kernel, out_shape=jax.ShapeDtypeStruct((COLS, SLAB), F32),...  118 us
    pallas_call x1, Pallas kernels, turned_back(): pl.pallas_call(turn_kernel, grid=(COLS // 2 // 16,), out_shape=jax.ShapeD...  3.67 us

profile of v3, /device:TPU:0, one launch (start us, length us, event | category | flops | bytes accessed | tf_op | source)
XLA Modules:
  0.0 122.0 jit_solution(10269343648714632019)
XLA Ops:
  0.0 118.3 %shard_map.55 = f32[128,2048]{1,0:T(8,128)} custom-call(f32[128,2048]{1,0:T(8,128)} %bitcast.7, f32[2,2048,256]{2,1,0:T(8,128)} %psi.1, f32[16,128]{1,0:T(8,128)} %bitcast.8, s32[2]{0:T(128)} %panels_hbm.1, s32[16]{0:T(128)} %offsets.1), custom_call_target="tpu_custom_call" | custom-call | tf_op jit(solution)/shard_map/pallas_call | solution.py:470
  118.3 3.7 %shard_map.56 = f32[2,64,2048]{2,1,0:T(8,128)} custom-call(s32[16]{0:T(128)} %offsets.1, f32[2,64,2048]{2,1,0:T(8,128)} %bitcast.6), custom_call_target="tpu_custom_call" | custom-call | tf_op jit(solution)/shard_map/pallas_call | solution.py:523

commit v4 on v3

--- a/solution.py
+++ b/solution.py
@@ -16,6 +16,10 @@
 PIECES = (0, 64, 256, 512, 640, HALF)
 LAST = PIECES[-2]
 L2, L1 = HALF // 2, BOTH // 2
+ORDER = (
+    (0, 0), (1, 0), (0, 1), (2, 0), (1, 1), (0, 2), (3, 0), (2, 1), (1, 2), (4, 0), (3, 1), (2, 2),
+    (5, 0), (4, 1), (6, 0), (3, 2), (5, 1), (4, 2), (5, 2),
+)
 NT = (((1,), (1,)), ((), ()))
 
 
@@ -38,7 +42,7 @@
 
 def kernel(
     raw_hbm, psi, table_hbm, panels_hbm, offsets_hbm, out,
-    raw, table, panels, offsets, at, psi_o, psi_p, a_v, a_hi, a_lo, o_hi, o_lo, p_hi, p_lo, ws, wv, m, w, c2, c1,
+    raw, table, panels, offsets, out_v, at, psi_o, psi_p, a_v, a_hi, a_lo, o_hi, o_lo, p_hi, p_lo, ws, wv, m, w, c2, c1,
     r0, r1, r2, s, rl2, rl1, fin2, fin1, zin, zg,
     local_sem, a_s, a_r, p_s, p_r, g_s, g_r, c_s, c_r,
 ):
@@ -232,9 +236,11 @@
             total = term if total is None else total + term
         return rows, total
 
+    keep_piece(3)
+
     def early(rel, _):
         own_bands(rel)
-        rows, total = pair_bands(block_rows(rel), 0, PIECES[3])
+        rows, total = pair_bands(block_rows(rel), 0, LAST)
         m[p, rows, :] = total
         return 0
 
@@ -243,14 +249,6 @@
         copy.wait_recv()
     keep_columns(a_v[0, p], 0, p)
     lax.fori_loop(0, 1, early, 0)
-    keep_piece(3)
-
-    def later(rel, _):
-        rows, total = pair_bands(block_rows(rel), PIECES[3], LAST)
-        m[p, rows, :] = m[p, rows, :] + total
-        return 0
-
-    lax.fori_loop(0, 4, later, 0)
     keep_piece(4)
 
     G = (g_s, g_r)
@@ -395,88 +393,104 @@
     def step5(n):
         landed(n)
         if n == 0:
-            both, alone = corrections(0)
-            alone(0)
-            alone(1)
-            send_relay(0)
-            send_relay(1)
-            both(0)
-            both(1)
-            to_pair(0)
+            _, alone = corrections(0)
+            for way, _, to in ways:
+                alone(way)
+                for i in (0, 1):
+                    relay[way, i] = send(piece(0, i, way), rl2.at[way, i], C, way * 3 + i, to)
         elif n == 1:
+            work = {rel: corrections(rel) for _, rel, _ in ways}
             for way, rel, _ in ways:
-                both, alone = corrections(rel)
+                work[rel][1](1 - way)
+                send_final(way, 0, 1 - way)
+            for way, rel, _ in ways:
+                work[rel][1](way)
+                send_held(way, 0)
+            for way in (0, 1):
+                send_final(way, 1, 1 - way)
+            for way in (0, 1):
+                send_held(way, 1)
+            summed_over_pair(0)
+            send_relay(2)
+            for _, rel, _ in ways:
+                both, _ = work[rel]
                 both(0)
                 both(1)
                 to_pair(rel)
-                alone(1 - way)
-                send_final(way, 0, 1 - way)
-                alone(way)
-            summed_over_pair(0)
-            send_relay(2)
-            for i in (0, 1):
-                for way in (0, 1):
-                    if i > 0:
-                        send_final(way, i, 1 - way)
-                for way in (0, 1):
-                    send_held(way, i)
         else:
             both, alone = corrections(3)
             both(0)
             both(1)
             to_pair(3)
+            alone(0)
+            alone(1)
             for way, rel, _ in ways:
                 summed_over_pair(rel)
                 send_final(way, 2, 1 - way)
             for way in (0, 1):
                 send_held(way, 2)
-            alone(0)
-            alone(1)
-
-    steps = (step0, step1, step2, step3, step4, step5)
-    for t in range(len(steps) + len(chunks) - 1):
-        for n in range(len(chunks)):
-            if 0 <= t - n < len(steps):
-                steps[t - n](n)
+
+    def step6(n):
+        if n == 0:
+            both, _ = corrections(0)
+            both(0)
+            both(1)
+            to_pair(0)
+
+    steps = (step0, step1, step2, step3, step4, step5, step6)
+    for step, n in ORDER:
+        steps[step](n)
 
     def arrived(i, l):
         final[0, i, l].wait_recv()
         final[1, i, l].wait_recv()
         return piece(3, i, l)[...] + (final_slot(0, i, l)[...] + final_slot(1, i, l)[...])
 
-    across = []
+    across, written = [], []
+
+    def write(first, length, value):
+        lanes = pl.ds(first, length)
+        out_v[:, lanes] = value
+        copy = pltpu.make_async_copy(out_v.at[:, lanes], out.at[:, lanes], local_sem.at[6 + len(written)])
+        copy.start()
+        written.append(copy)
+
     for l in (0, 1):
         c2[3, p, l] = arrived(0, l)
         across.append(send(c2.at[3, p, l], zin.at[l], C, 18 + l, pair))
     for l in (0, 1):
-        lanes = pl.ds(pl.multiple_of(o * HALF + l * L2, 128), L2)
-        out[:, lanes] = at[o, :, l * L2 : (l + 1) * L2] - arrived(1, l)
+        value = at[o, :, l * L2 : (l + 1) * L2] - arrived(1, l)
+        write(pl.multiple_of(o * HALF + l * L2, 128), L2, value)
+    for l in (0, 1):
+        across[l].wait_recv()
+        value = at[p, :, l * L2 : (l + 1) * L2] - zin[l]
+        write(pl.multiple_of(p * HALF + l * L2, 128), L2, value)
     summed_over_pair(3)
     for l in (0, 1):
         first = HALF + l * L1
-        out[:, HALF + first : HALF + first + L1] = at[o, :, first : first + L1] - arrived(2, l)
-    for l in (0, 1):
-        across[l].wait_recv()
-        lanes = pl.ds(pl.multiple_of(p * HALF + l * L2, 128), L2)
-        out[:, lanes] = at[p, :, l * L2 : (l + 1) * L2] - zin[l]
-
+        value = at[o, :, first : first + L1] - arrived(2, l)
+        write(HALF + first, L1, value)
+
+    for copy in written:
+        copy.wait()
     for copy in sent:
         copy.wait_send()
 
 
 def projected(raw, psi, table, panels, offsets):
     dma = pltpu.SemaphoreType.DMA
-    vmem, hbm = pl.BlockSpec(memory_space=pltpu.VMEM), pl.BlockSpec(memory_space=pltpu.HBM)
+    hbm = pl.BlockSpec(memory_space=pltpu.HBM)
     return pl.pallas_call(
         kernel,
         out_shape=jax.ShapeDtypeStruct((COLS, SLAB), F32),
         in_specs=[hbm] * 5,
-        out_specs=vmem,
+        out_specs=hbm,
         scratch_shapes=[
             pltpu.VMEM((COLS, SLAB), F32),
             pltpu.VMEM((16, PANEL), F32),
             pltpu.SMEM((2,), jnp.int32),
             pltpu.SMEM((16,), jnp.int32),
+            pltpu.VMEM((COLS, SLAB), F32),
             pltpu.VMEM((2, COLS, MINE), F32),
             pltpu.VMEM((2, MINE, BANDS), F32),
             pltpu.VMEM((2, HALF, BANDS), F32),
@@ -503,7 +517,7 @@
             pltpu.VMEM((2, 2, COLS, L1), F32),
             pltpu.VMEM((2, COLS, L2), F32),
             pltpu.VMEM((4, 2, COLS, L1), F32),
-            dma((6,)), dma((15,)), dma((15,)), dma((5,)), dma((5,)),
+            dma((12,)), dma((15,)), dma((15,)), dma((5,)), dma((5,)),
             dma((60,)), dma((60,)), dma((24,)), dma((24,)),
         ],
         compiler_params=pltpu.CompilerParams(
@@ -519,10 +533,10 @@
 
 
 def turned_back(value, offsets):
-    block = pl.BlockSpec((2, 16, SLAB), lambda k: (0, k, 0))
+    block = pl.BlockSpec((2, 32, SLAB), lambda k: (0, k, 0))
     return pl.pallas_call(
         turn_kernel,
-        grid=(COLS // 2 // 16,),
+        grid=(COLS // 2 // 32,),
         out_shape=jax.ShapeDtypeStruct((2, COLS // 2, SLAB), F32),
         in_specs=[pl.BlockSpec(memory_space=pltpu.SMEM), block],
         out_specs=block,

time: 122 us -> 126 us (1.033)
  Pallas kernels: 122 us -> 126 us
    pallas_call x1, Pallas kernels: 118 us -> 124 us  [projected(): pl.pallas_call(kernel, out_shape=jax.ShapeDtypeStruct((COLS, SLAB), F32),...]
    pallas_call x1, Pallas kernels: 3.67 us -> 2.38 us  [turned_back(): pl.pallas_call(turn_kernel, grid=(COLS // 2 // 32,), out_shape=jax.ShapeD...]
where the time goes in v4:
time: 126 us
  Pallas kernels  126 us (100%)
    pallas_call x1, Pallas kernels, projected(): pl.pallas_call(kernel, out_shape=jax.ShapeDtypeStruct((COLS, SLAB), F32),...  124 us

profile of v4, /device:TPU:0, one launch (start us, length us, event | category | flops | bytes accessed | tf_op | source)
XLA Modules:
  0.0 126.1 jit_solution(17133478141048248342)
XLA Ops:
  0.0 123.8 %shard_map.55 = f32[128,2048]{1,0:T(8,128)} custom-call(f32[128,2048]{1,0:T(8,128)} %bitcast.7, f32[2,2048,256]{2,1,0:T(8,128)} %psi.1, f32[16,128]{1,0:T(8,128)} %bitcast.8, s32[2]{0:T(128)} %panels_hbm.1, s32[16]{0:T(128)} %offsets.1), custom_call_target="tpu_custom_call" | custom-call | tf_op jit(solution)/shard_map/pallas_call | solution.py:483
  123.8 2.4 %shard_map.56 = f32[2,64,2048]{2,1,0:T(8,128)} custom-call(s32[16]{0:T(128)} %offsets.1, f32[2,64,2048]{2,1,0:T(8,128)} %bitcast.6), custom_call_target="tpu_custom_call" | custom-call | tf_op jit(solution)/shard_map/pallas_call | solution.py:537

commit v5 on v3

--- a/solution.py
+++ b/solution.py
@@ -396,14 +396,16 @@
         landed(n)
         if n == 0:
             both, alone = corrections(0)
-            alone(0)
-            alone(1)
-            send_relay(0)
-            send_relay(1)
+            for way, _, to in ways:
+                alone(way)
+                for i in (0, 1):
+                    relay[way, i] = send(piece(0, i, way), rl2.at[way, i], C, way * 3 + i, to)
             both(0)
             both(1)
             to_pair(0)
         elif n == 1:
+            summed_over_pair(0)
+            send_relay(2)
             for way, rel, _ in ways:
                 both, alone = corrections(rel)
                 both(0)
@@ -412,8 +414,6 @@
                 alone(1 - way)
                 send_final(way, 0, 1 - way)
                 alone(way)
-            summed_over_pair(0)
-            send_relay(2)
             for i in (0, 1):
                 for way in (0, 1):
                     if i > 0:
@@ -519,10 +519,10 @@
 
 
 def turned_back(value, offsets):
-    block = pl.BlockSpec((2, 16, SLAB), lambda k: (0, k, 0))
+    block = pl.BlockSpec((2, 32, SLAB), lambda k: (0, k, 0))
     return pl.pallas_call(
         turn_kernel,
-        grid=(COLS // 2 // 16,),
+        grid=(COLS // 2 // 32,),
         out_shape=jax.ShapeDtypeStruct((2, COLS // 2, SLAB), F32),
         in_specs=[pl.BlockSpec(memory_space=pltpu.SMEM), block],
         out_specs=block,

time: 122 us -> 120 us (0.984)
  Pallas kernels: 122 us -> 120 us
    pallas_call x1, Pallas kernels: 3.67 us -> 2.38 us  [turned_back(): pl.pallas_call(turn_kernel, grid=(COLS // 2 // 32,), out_shape=jax.ShapeD...]
where the time goes in v5:
time: 120 us
  Pallas kernels  120 us (100%)
    pallas_call x1, Pallas kernels, projected(): pl.pallas_call(kernel, out_shape=jax.ShapeDtypeStruct((COLS, SLAB), F32),...  118 us

profile of v5, /device:TPU:0, one launch (start us, length us, event | category | flops | bytes accessed | tf_op | source)
XLA Modules:
  0.0 119.9 jit_solution(14383962114820138595)
XLA Ops:
  0.0 117.5 %shard_map.55 = f32[128,2048]{1,0:T(8,128)} custom-call(f32[128,2048]{1,0:T(8,128)} %bitcast.7, f32[2,2048,256]{2,1,0:T(8,128)} %psi.1, f32[16,128]{1,0:T(8,128)} %bitcast.8, s32[2]{0:T(128)} %panels_hbm.1, s32[16]{0:T(128)} %offsets.1), custom_call_target="tpu_custom_call" | custom-call | tf_op jit(solution)/shard_map/pallas_call | solution.py:470
  117.5 2.4 %shard_map.56 = f32[2,64,2048]{2,1,0:T(8,128)} custom-call(s32[16]{0:T(128)} %offsets.1, f32[2,64,2048]{2,1,0:T(8,128)} %bitcast.6), custom_call_target="tpu_custom_call" | custom-call | tf_op jit(solution)/shard_map/pallas_call | solution.py:523

commit v6 on v5

--- a/solution.py
+++ b/solution.py
@@ -38,7 +38,7 @@
 
 def kernel(
     raw_hbm, psi, table_hbm, panels_hbm, offsets_hbm, out,
-    raw, table, panels, offsets, at, psi_o, psi_p, a_v, a_hi, a_lo, o_hi, o_lo, p_hi, p_lo, ws, wv, m, w, c2, c1,
+    raw, table, panels, offsets, out_v, at, psi_o, psi_p, a_v, a_hi, a_lo, o_hi, o_lo, p_hi, p_lo, ws, wv, m, w, c2, c1,
     r0, r1, r2, s, rl2, rl1, fin2, fin1, zin, zg,
     local_sem, a_s, a_r, p_s, p_r, g_s, g_r, c_s, c_r,
 ):
@@ -345,6 +345,8 @@
                 total = term if total is None else total + term
             c1[rel, 0, l] = total[:COLS]
             c1[rel, 1, l] = total[COLS:]
+            copy = send(c1.at[rel, p, l], zg.at[rel, l], C, 20 + rel * 2 + l, pair)
+            pairs.setdefault(rel, []).append(copy)
 
         def alone(l):
             total = None
@@ -366,7 +368,8 @@
         return (c2.at[rel, p, l], c2.at[rel, o, l], c1.at[rel, o, l])[i]
 
     def summed_over_pair(rel):
-        pairs[rel].wait_recv()
+        for copy in pairs[rel]:
+            copy.wait_recv()
         c1[rel, o] = c1[rel, o] + zg[rel]
 
     def final_slot(way, i, l):
@@ -377,9 +380,6 @@
         final[way, i, l] = send(
             piece(rel, i, l), final_slot(way, i, l), C, 6 + way * 6 + i * 2 + l, to
         )
-
-    def to_pair(rel):
-        pairs[rel] = send(c1.at[rel, p], zg.at[rel], C, 20 + rel, pair)
 
     def send_relay(i):
         for way, _, to in ways:
@@ -402,15 +402,14 @@
                     relay[way, i] = send(piece(0, i, way), rl2.at[way, i], C, way * 3 + i, to)
             both(0)
             both(1)
-            to_pair(0)
         elif n == 1:
-            summed_over_pair(0)
-            send_relay(2)
             for way, rel, _ in ways:
                 both, alone = corrections(rel)
                 both(0)
                 both(1)
-                to_pair(rel)
+                if way == 0:
+                    summed_over_pair(0)
+                    send_relay(2)
                 alone(1 - way)
                 send_final(way, 0, 1 - way)
                 alone(way)
@@ -424,7 +423,6 @@
             both, alone = corrections(3)
             both(0)
             both(1)
-            to_pair(3)
             for way, rel, _ in ways:
                 summed_over_pair(rel)
                 send_final(way, 2, 1 - way)
@@ -444,39 +442,51 @@
         final[1, i, l].wait_recv()
         return piece(3, i, l)[...] + (final_slot(0, i, l)[...] + final_slot(1, i, l)[...])
 
-    across = []
+    across, written = [], []
+
+    def write(first, length, value):
+        lanes = pl.ds(first, length)
+        out_v[:, lanes] = value
+        copy = pltpu.make_async_copy(out_v.at[:, lanes], out.at[:, lanes], local_sem.at[6 + len(written)])
+        copy.start()
+        written.append(copy)
+
     for l in (0, 1):
         c2[3, p, l] = arrived(0, l)
         across.append(send(c2.at[3, p, l], zin.at[l], C, 18 + l, pair))
     for l in (0, 1):
-        lanes = pl.ds(pl.multiple_of(o * HALF + l * L2, 128), L2)
-        out[:, lanes] = at[o, :, l * L2 : (l + 1) * L2] - arrived(1, l)
+        value = at[o, :, l * L2 : (l + 1) * L2] - arrived(1, l)
+        write(pl.multiple_of(o * HALF + l * L2, 128), L2, value)
     summed_over_pair(3)
     for l in (0, 1):
         first = HALF + l * L1
-        out[:, HALF + first : HALF + first + L1] = at[o, :, first : first + L1] - arrived(2, l)
+        value = at[o, :, first : first + L1] - arrived(2, l)
+        write(HALF + first, L1, value)
     for l in (0, 1):
         across[l].wait_recv()
-        lanes = pl.ds(pl.multiple_of(p * HALF + l * L2, 128), L2)
-        out[:, lanes] = at[p, :, l * L2 : (l + 1) * L2] - zin[l]
-
+        value = at[p, :, l * L2 : (l + 1) * L2] - zin[l]
+        write(pl.multiple_of(p * HALF + l * L2, 128), L2, value)
+
+    for copy in written:
+        copy.wait()
     for copy in sent:
         copy.wait_send()
 
 
 def projected(raw, psi, table, panels, offsets):
     dma = pltpu.SemaphoreType.DMA
-    vmem, hbm = pl.BlockSpec(memory_space=pltpu.VMEM), pl.BlockSpec(memory_space=pltpu.HBM)
+    hbm = pl.BlockSpec(memory_space=pltpu.HBM)
     return pl.pallas_call(
         kernel,
         out_shape=jax.ShapeDtypeStruct((COLS, SLAB), F32),
         in_specs=[hbm] * 5,
-        out_specs=vmem,
+        out_specs=hbm,
         scratch_shapes=[
             pltpu.VMEM((COLS, SLAB), F32),
             pltpu.VMEM((16, PANEL), F32),
             pltpu.SMEM((2,), jnp.int32),
             pltpu.SMEM((16,), jnp.int32),
+            pltpu.VMEM((COLS, SLAB), F32),
             pltpu.VMEM((2, COLS, MINE), F32),
             pltpu.VMEM((2, MINE, BANDS), F32),
             pltpu.VMEM((2, HALF, BANDS), F32),
@@ -503,8 +513,8 @@
             pltpu.VMEM((2, 2, COLS, L1), F32),
             pltpu.VMEM((2, COLS, L2), F32),
             pltpu.VMEM((4, 2, COLS, L1), F32),
-            dma((6,)), dma((15,)), dma((15,)), dma((5,)), dma((5,)),
-            dma((60,)), dma((60,)), dma((24,)), dma((24,)),
+            dma((12,)), dma((15,)), dma((15,)), dma((5,)), dma((5,)),
+            dma((60,)), dma((60,)), dma((28,)), dma((28,)),
         ],
         compiler_params=pltpu.CompilerParams(
             collective_id=0, has_side_effects=True, vmem_limit_bytes=62 * 1024 * 1024

time: 120 us -> 120 us (level)
  no operation moved by 1% of the time
where the time goes in v6:
time: 120 us
  Pallas kernels  120 us (100%)
    pallas_call x1, Pallas kernels, projected(): pl.pallas_call(kernel, out_shape=jax.ShapeDtypeStruct((COLS, SLAB), F32),...  117 us

profile of v6, /device:TPU:0, one launch (start us, length us, event | category | flops | bytes accessed | tf_op | source)
XLA Modules:
  0.0 119.8 jit_solution(17832690613657237610)
XLA Ops:
  0.0 117.4 %shard_map.55 = f32[128,2048]{1,0:T(8,128)} custom-call(f32[128,2048]{1,0:T(8,128)} %bitcast.7, f32[2,2048,256]{2,1,0:T(8,128)} %psi.1, f32[16,128]{1,0:T(8,128)} %bitcast.8, s32[2]{0:T(128)} %panels_hbm.1, s32[16]{0:T(128)} %offsets.1), custom_call_target="tpu_custom_call" | custom-call | tf_op jit(solution)/shard_map/pallas_call | solution.py:479
  117.4 2.4 %shard_map.56 = f32[2,64,2048]{2,1,0:T(8,128)} custom-call(s32[16]{0:T(128)} %offsets.1, f32[2,64,2048]{2,1,0:T(8,128)} %bitcast.6), custom_call_target="tpu_custom_call" | custom-call | tf_op jit(solution)/shard_map/pallas_call | solution.py:533
